TPU v7x, 256 devices: a whole 4x4x8 slice. The times are simulated.
256 devices in a mesh: dp: 128 (over y, x_lo, z, core), rep: 2 (over x_hi).
Axes of the slice: x: 4 (x_hi: 2, x_lo: 2; x = x_hi * 2 + x_lo), y: 4, z: 8, core: 2. Of those that a mesh axis runs over, the one named last changes fastest.
Arguments:
- gate_pre: bfloat16 [2, 16384, 5632], P(None, 'dp', 'rep'), may hold values from -8 to 8
- up_pre: bfloat16 [2, 16384, 5632], P(None, 'dp', 'rep'), may hold values from -6 to 6
- out_grad: bfloat16 [2, 16384, 1024], P(None, 'dp'), may hold values from -24 to 24
- master: float32 [1024, 5632], P('dp', 'rep'), may hold values from -0.078125 to 0.078125
- moment_one: float32 [1024, 5632], P('dp', 'rep'), may hold values from -0.02 to 0.02
- moment_two: float32 [1024, 5632], P('dp', 'rep'), may hold values from 1e-06 to 1e-05
Outputs:
- layer_out: bfloat16 [2, 16384, 1024], P(None, 'dp', 'rep')
- gate_grad: bfloat16 [2, 16384, 5632], P(None, 'dp', 'rep')
- up_grad: bfloat16 [2, 16384, 5632], P(None, 'dp', 'rep')
- master_new: float32 [1024, 5632], P('dp', 'rep')
- moment_one_new: float32 [1024, 5632], P('dp', 'rep')
- moment_two_new: float32 [1024, 5632], P('dp', 'rep')
All inputs are finite; a program needn't handle non-finite values.
Results may differ from a plain program's by a relative error of at most 0.0048.
The roundings to bfloat16 on the way count: a program that leaves them out, or rounds other values in their place, can miss the bound.
Values may be sent and summed in bfloat16 or wider, within the bound.
A program may use at most 128 MiB of HBM per device.

v0:
```python
import jax
import jax.numpy as jnp
from jax import lax
from jax.sharding import Mesh
from jax.sharding import PartitionSpec as P

DP = ("dp_0", "dp_1", "dp_2", "dp_3")


first_power = 2.6561398887587544e-05
second_power = 0.005920529220333997


def in_blocks(x, dim, peers):
    before, after = (x.shape[:dim], x.shape[dim + 1 :])
    return jnp.moveaxis(x.reshape(*before, peers, -1, *after), dim, 0)


def sent_and_summed(x, axis, dim):
    peers = lax.axis_size(axis)
    parts = lax.all_to_all(in_blocks(x, dim, peers), axis, 0, 0, tiled=True)
    return jnp.sum(parts, axis=0)


def sum_by_chip_2(x, chips, core, dim):
    sizes = (lax.axis_size(chips), lax.axis_size(core))
    parts = in_blocks(x, dim, sizes[0] * sizes[1])
    inside = parts.shape[1:]
    parts = parts.reshape(*sizes, *inside).swapaxes(0, 1).reshape(-1, *inside)
    parts = lax.psum_scatter(parts, core, scatter_dimension=0, tiled=True)
    return lax.psum_scatter(parts, chips, scatter_dimension=0, tiled=True)[0]


def grad_rows(cotangent, hidden):
    return lax.dot_general(
        cotangent, hidden, (((0,), (0,)), ((), ())), preferred_element_type=jnp.float32
    )


def on_device(gate_pre, up_pre, out_grad, master, moment_one, moment_two):
    shard_bf = master.astype(jnp.bfloat16)
    weights = lax.all_gather(shard_bf, DP, axis=0, tiled=True)
    micro = gate_pre.shape[0]
    total = micro * gate_pre.shape[1] * lax.axis_size(DP)
    own_rows = master.shape[0]
    outs_list = []
    gate_list = []
    up_list = []
    hidden_list = []
    grad_sum = None
    for index in range(micro):
        gate = gate_pre[index].astype(jnp.float32)
        up_val = up_pre[index].astype(jnp.float32)
        sig = jax.nn.sigmoid(gate)
        hidden = (gate * sig * up_val).astype(jnp.bfloat16)
        hidden_list.append(hidden)
        partial_out = lax.dot_general(
            hidden, weights, (((1,), (1,)), ((), ())), preferred_element_type=jnp.float32
        )
        outs_list.append(sent_and_summed(partial_out, "rep", 1).astype(jnp.bfloat16))
        hid_grad = jnp.dot(out_grad[index], weights, preferred_element_type=jnp.float32)
        gate_list.append(
            (hid_grad * up_val * sig * (1.0 + gate * (1.0 - sig))).astype(jnp.bfloat16)
        )
        up_list.append((hid_grad * gate * sig).astype(jnp.bfloat16))

        def single_term(start, count, cotangent=out_grad[index], current=hidden):
            return grad_rows(cotangent, current)

        shard_grad = sum_by_chip_2(
            single_term(
                jnp.int32(0),
                own_rows * lax.axis_size(("dp_0", "dp_1", "dp_2")) * lax.axis_size("dp_3"),
            ),
            ("dp_0", "dp_1", "dp_2"),
            "dp_3",
            0,
        )
        grad_sum = shard_grad if grad_sum is None else grad_sum + shard_grad
    main_grad = grad_sum / jnp.float32(total)
    first = 0.9 * moment_one + 0.1 * main_grad
    second = 0.95 * moment_two + 0.05 * main_grad * main_grad
    update = first / (1.0 - first_power) / (jnp.sqrt(second / (1.0 - second_power)) + 1e-08)
    master_new = master - 0.003 * (update + 0.1 * master)
    return (
        jnp.stack(outs_list),
        jnp.stack(gate_list),
        jnp.stack(up_list),
        master_new,
        first,
        second,
    )


def solution(mesh):
    torus = Mesh(
        mesh.devices.reshape(4, 2, 8, 2, mesh.shape["rep"]), ("dp_0", "dp_1", "dp_2", "dp_3", "rep")
    )
    return jax.shard_map(
        on_device,
        mesh=torus,
        in_specs=(
            P(None, DP, "rep"),
            P(None, DP, "rep"),
            P(None, DP, None),
            P(DP, "rep"),
            P(DP, "rep"),
            P(DP, "rep"),
        ),
        out_specs=(
            P(None, DP, "rep"),
            P(None, DP, "rep"),
            P(None, DP, "rep"),
            P(DP, "rep"),
            P(DP, "rep"),
            P(DP, "rep"),
        ),
        check_vma=False,
    )
```

profile of v0, /device:TPU:1, one launch (start us, length us, event | category | flops | bytes accessed | tf_op | source)
XLA Modules:
  0.0 639.2 jit_solution(1135383162872716029)
XLA Ops:
  7.2 0.0 reduce-scatter.5.cloned.1.call-start
  7.2 3.2 fusion.37
  10.5 6.0 convolution_add_fusion
  16.5 9.5 %copy.12 = f32[2,64,8,2816]{3,2,1,0:T(8,128)} copy(f32[2,64,8,2816]{3,2,0,1:T(8,128)} %bitcast.143) | data formatting | bytes 23068672 | tf_op jit(solution)/shard_map/add | solution.py:79
  26.1 0.0 reduce-scatter.3.cloned.1.call-start
  26.1 29.7 %reduce-scatter.5.cloned.1.call-done = f32[64,8,2816]{2,1,0:T(8,128)} async-done(((f32[128,8,2816]{2,1,0:T(8,128)}), f32[64,8,2816]{2,1,0:T(8,128)}) %reduce-scatter.5.cloned.1.call-update) | async-done | bytes 5767184 | tf_op jit(solution)/shard_map/reduce_scatter | solution.py:30
  55.8 0.0 reduce-scatter.3.cloned.1.call-update
  55.8 0.0 all-gather.2.cloned.1.call-start
  55.8 284.1 %reduce-scatter.3.cloned.1.call-done = f32[1,8,2816]{2,1,0:T(8,128)} async-done(((f32[64,8,2816]{2,1,0:T(8,128)}), f32[1,8,2816]{2,1,0:T(8,128)}) %reduce-scatter.3.cloned.1.call-update) | async-done | bytes 90128 | tf_op jit(solution)/shard_map/reduce_scatter | solution.py:31
  339.9 1.6 multiply_subtract_fusion
  341.6 0.0 all-gather.2.cloned.1.call-update
  341.6 258.5 %all-gather.2.cloned.1.call-done = bf16[1024,2816]{1,0:T(8,128)(2,1)} async-done(((bf16[8,2816]{1,0:T(8,128)(2,1)}), bf16[1024,2816]{1,0:T(8,128)(2,1)}) %all-gather.2.cloned.1.call-update) | async-done | bytes 5767184 | tf_op jit(solution)/shard_map/all_gather | solution.py:42
  600.1 5.4 convolution_bitcast_fusion
  605.5 4.0 all-to-all-start.1
  609.6 3.8 fusion.44
  613.4 0.1 slice-done.1
  613.5 0.4 copy-done.2
  613.9 0.1 copy-done.4
  614.0 3.1 fusion.40
  617.1 2.8 convolution_bitcast_fusion.1
  619.9 4.4 all-to-all-start
  624.3 3.4 pad_maximum_fusion
  627.7 4.2 all-to-all-done
  631.9 0.7 pad_maximum_fusion.2
  (24 shorter events, 0.1 us)
Async XLA Ops:
  7.2 3.3 copy-start
  7.2 3.3 copy-start.1
  7.2 3.3 copy-start.3
  7.2 48.6 %reduce-scatter.5.cloned.1.call-start = ((), (), s32[]{:S(2)}) async-start(), calls=%async_computation.6 | async-start | bytes 17301504 | tf_op jit(solution)/shard_map/reduce_scatter | solution.py:30
  26.1 313.9 %reduce-scatter.3.cloned.1.call-start = ((), (), s32[]{:S(2)}) async-start(), calls=%async_computation.5 | async-start | bytes 5857280 | tf_op jit(solution)/shard_map/reduce_scatter | solution.py:31
  55.8 284.2 %copy-start.6 = (f32[8,2816]{1,0:T(8,128)S(1)}, f32[8,2816]{1,0:T(8,128)}, u32[]{:S(2)}) copy-start(f32[8,2816]{1,0:T(8,128)} %param.9) | copy-start | bytes 270340
  55.8 284.2 %copy-start.7 = (f32[8,2816]{1,0:T(8,128)S(1)}, f32[8,2816]{1,0:T(8,128)}, u32[]{:S(2)}) copy-start(f32[8,2816]{1,0:T(8,128)} %param.10) | copy-start | bytes 270340
  55.8 284.2 %copy-start.8 = (f32[8,2816]{1,0:T(8,128)S(1)}, f32[8,2816]{1,0:T(8,128)}, u32[]{:S(2)}) copy-start(f32[8,2816]{1,0:T(8,128)} %param.11) | copy-start | bytes 270340
  55.8 544.3 %all-gather.2.cloned.1.call-start = ((), (), s32[]{:S(2)}) async-start(), calls=%async_computation.4 | async-start | bytes 5812224 | tf_op jit(solution)/shard_map/all_gather | solution.py:42
  605.5 7.8 %slice-start = ((s8[5767168]{0:T(1024)(128)(4,1)}), s8[1572864]{0:T(1024)(128)(4,1)S(1)}, s32[]{:S(2)}) async-start(s8[5767168]{0:T(1024)(128)(4,1)} %bitcast.146), calls=%async_computation.7 | async-start | bytes 3145728
  605.5 14.3 %all-to-all-start.1 = ((f32[2,128,512]{2,1,0:T(8,128)}), f32[2,128,512]{2,1,0:T(8,128)S(1)}, u32[]{:S(2)}, u32[]{:S(2)}) async-start(f32[2,128,512]{2,1,0:T(8,128)} %convolution_bitcast_fusion), calls=%async_computation.1 | async-start | bytes 1048576 | tf_op jit(solution)/shard_map/all_to_all | solution.py:21
  609.6 3.9 slice-start.1
  609.6 4.4 copy-start.2
  609.6 4.5 copy-start.4
  619.9 4.4 copy-start.5
  619.9 12.0 %all-to-all-start = ((f32[2,128,512]{2,1,0:T(8,128)}), f32[2,128,512]{2,1,0:T(8,128)S(1)}, u32[]{:S(2)}, u32[]{:S(2)}) async-start(f32[2,128,512]{2,1,0:T(8,128)} %convolution_bitcast_fusion.1), calls=%async_computation | async-start | bytes 1048576 | tf_op jit(solution)/shard_map/all_to_all | solution.py:21
Sparse Core Ops, SparseCore 0:
  26.2 29.5 reduce-scatter.4
  58.3 281.5 reduce-scatter.2
  342.4 257.6 all-gather.1
where the time goes:
time: 642 us; the launch traced here: 639 us
  waiting for transfers between devices  576 us (90%)
  matrix products  24.3 us (4%)
  between operations  13.8 us (2%)
  local copies, waits for them, and re-layouts  10.2 us (2%)
  starting transfers between devices  8.49 us (1%)
    reduce_scatter x1, waiting for transfers between devices, sum_by_chip_2(): return lax.psum_scatter(parts, chips, scatter_dimension=0, tiled=True)[0]  284 us
    all_gather x1, waiting for transfers between devices, on_device(): weights = lax.all_gather(shard_bf, DP, axis=0, tiled=True)  259 us
    reduce_scatter x1, waiting for transfers between devices, sum_by_chip_2(): parts = lax.psum_scatter(parts, core, scatter_dimension=0, tiled=True)  29.7 us
  transfers between devices with their start and end apart: 5, of which 4 were waited for; matrix products, arithmetic and copies ran while one was open for 2% of the time, Pallas kernels for 0%

commit v1 on v0

v1 whole, which is shorter than its diff:
```python
import jax
import jax.numpy as jnp
from jax import lax
from jax.experimental import pallas as pl
from jax.experimental.pallas import tpu as pltpu
from jax.sharding import Mesh
from jax.sharding import PartitionSpec as P

DP = ("dp_0", "dp_1", "dp_2", "dp_3")
NY, NX, NZ, NC = 4, 2, 8, 2

first_power = 2.6561398887587544e-05
second_power = 0.005920529220333997

F32 = jnp.float32
BF = jnp.bfloat16
D = 1024
FF = 2816
HALF = 1408
TOK = 256
A = (0, 512)
B = (512, 512)
C = (1024, 384)
BC = (512, 896)


def cols(r):
    return pl.ds(r[0], r[1])


def kernel(
    gate_ref, up_ref, og_ref, master_ref, one_ref, two_ref,
    out_ref, gg_ref, ug_ref, master_out, one_out, two_out,
    W, G, hid2, hidO, ogP, ogT, mP, hg, acc, fin, finP, lo_s, lo_r,
    sa1, ra1, sa2, ra2, sa3, ra3, sa4, ra4,
    sb1, rb1, sb2, rb2, sb3, rb3, sb4, rb4,
    sc1, rc1, sc2, rc2, sc3, rc3, sc4, rc4,
    ssem, rsem,
):
    y = lax.axis_index("dp_0")
    x = lax.axis_index("dp_1")
    z = lax.axis_index("dp_2")
    c = lax.axis_index("dp_3")
    r = lax.axis_index("rep")
    oc = 1 - c
    ox = 1 - x

    def dy(o):
        return {"dp_0": lax.rem(y + (o % NY), NY)}

    def dz(o):
        return {"dp_2": lax.rem(z + (o % NZ), NZ)}

    def zz(o):
        return lax.rem(z + (o % NZ), NZ)

    def yy(o):
        return lax.rem(y + (o % NY), NY)

    dx = {"dp_1": ox}
    dc = {"dp_3": oc}
    dr = {"rep": 1 - r}

    peers = [dc, dx, dr] + [dy(o) for o in range(1, NY)] + [dz(o) for o in range(1, NZ)]
    bar = pltpu.get_barrier_semaphore()
    for p in peers:
        pl.semaphore_signal(bar, inc=1, device_id=p, device_id_type=pl.DeviceIdType.MESH)
    pl.semaphore_wait(bar, len(peers))

    sent = []
    slots = {}

    def slot(name):
        if name not in slots:
            slots[name] = len(slots)
        return slots[name]

    def rc(name, src, dst, dev):
        k = slot(name)
        return pltpu.make_async_remote_copy(
            src_ref=src, dst_ref=dst, send_sem=ssem.at[k], recv_sem=rsem.at[k],
            device_id=dev, device_id_type=pl.DeviceIdType.MESH,
        )

    def send(name, src, dst, dev):
        d = rc(name, src, dst, dev)
        d.start()
        sent.append(d)

    def recv(name, dst, dev):
        rc(name, dst, dst, dev).wait_recv()

    def hidden_rows(half, out, out_base):
        off = pl.multiple_of(half * HALF, 128)

        def body(i, _):
            rows = pl.ds(pl.multiple_of(i * 16, 16), 16)
            g = gate_ref[rows, pl.ds(off, HALF)].astype(F32)
            u = up_ref[rows, pl.ds(off, HALF)].astype(F32)
            s = jax.nn.sigmoid(g)
            out[pl.ds(pl.multiple_of(out_base + i * 16, 16), 16), :] = (g * s * u).astype(BF)
            return 0

        lax.fori_loop(0, TOK // 16, body, 0)

    send("m", master_ref.at[:, pl.ds(pl.multiple_of(oc * HALF, 128), HALF)], mP, dc)
    send("og", og_ref, ogP, dc)

    recv("m", mP, dc)
    mine = master_ref[:, pl.ds(pl.multiple_of(c * HALF, 128), HALF)]
    theirs = mP[...]
    first_core = c == 0
    W[c, y, x, z] = jnp.concatenate(
        [jnp.where(first_core, mine, theirs), jnp.where(first_core, theirs, mine)], axis=0
    ).astype(BF)

    def Wb(*idx):
        return W.at[(c,) + idx]

    send("Ax", Wb(y, x, z, slice(None), cols(A)), Wb(y, x, z, slice(None), cols(A)), dx)
    for o in (4, 3, 5, 2, 6, 1, 7):
        ref = Wb(y, x, z, slice(None), cols(BC))
        send(f"Zd{o}", ref, ref, dz(o))

    hidden_rows(oc, hidO, 0)
    send("h", hidO, hid2.at[pl.ds(TOK, TOK)], dc)
    hidden_rows(c, hid2, 0)
    for b in range(4):
        ogT[b, :, 0:TOK] = og_ref[:, b * 256 : (b + 1) * 256].T

    allr = slice(None)

    def A1():
        recv("Ax", Wb(y, ox, z, allr, cols(A)), dx)
        ref = Wb(y, allr, z, allr, cols(A))
        for o in (2, 1, 3):
            send(f"Ay{o}", ref, ref, dy(o))

    def A2():
        for o in (1, 3, 2):
            recv(f"Ay{o}", Wb(yy(-o), allr, z, allr, cols(A)), dy(-o))
        ref = Wb(allr, allr, z, allr, cols(A))
        send("Az1R", ref, ref, dz(1))
        send("Az1L", ref, ref, dz(-1))

    def A3(step):
        ref = Wb(allr, allr, zz(-step), allr, cols(A))
        recv(f"Az{step}R", ref, dz(-1))
        if step < 3:
            send(f"Az{step + 1}R", ref, ref, dz(1))
        else:
            h = Wb(pl.ds(0, 2), allr, zz(-3), allr, cols(A))
            send("Az4R", h, h, dz(1))
        ref = Wb(allr, allr, zz(step), allr, cols(A))
        recv(f"Az{step}L", ref, dz(1))
        if step < 3:
            send(f"Az{step + 1}L", ref, ref, dz(-1))
        else:
            h = Wb(pl.ds(2, 2), allr, zz(3), allr, cols(A))
            send("Az4L", h, h, dz(-1))

    def A6():
        recv("Az4R", Wb(pl.ds(0, 2), allr, zz(4), allr, cols(A)), dz(-1))
        recv("Az4L", Wb(pl.ds(2, 2), allr, zz(4), allr, cols(A)), dz(1))
        ref = Wb(allr, allr, allr, allr, cols(A))
        send("DA", ref, ref, dc)

    def BC1():
        for o in (1, 7, 2, 6, 3, 5, 4):
            recv(f"Zd{o}", Wb(y, x, zz(-o), allr, cols(BC)), dz(-o))
        ref = Wb(y, x, allr, allr, cols(B))
        send("Bx", ref, ref, dx)
        ref = Wb(y, x, allr, allr, cols(C))
        send("Cy1R", ref, ref, dy(1))
        send("Cy1L", ref, ref, dy(-1))

    def B2():
        recv("Bx", Wb(y, ox, allr, allr, cols(B)), dx)
        ref = Wb(y, allr, allr, allr, cols(B))
        send("By1R", ref, ref, dy(1))
        send("By1L", ref, ref, dy(-1))

    def B3():
        recv("By1R", Wb(yy(-1), allr, allr, allr, cols(B)), dy(-1))
        ref = Wb(yy(-1), 0, allr, allr, cols(B))
        send("By2R", ref, ref, dy(1))
        recv("By1L", Wb(yy(1), allr, allr, allr, cols(B)), dy(1))
        ref = Wb(yy(1), 1, allr, allr, cols(B))
        send("By2L", ref, ref, dy(-1))

    def B4():
        recv("By2R", Wb(yy(2), 0, allr, allr, cols(B)), dy(-1))
        recv("By2L", Wb(yy(2), 1, allr, allr, cols(B)), dy(1))
        ref = Wb(allr, allr, allr, allr, cols(B))
        send("DB", ref, ref, dc)

    def C2():
        recv("Cy1R", Wb(yy(-1), x, allr, allr, cols(C)), dy(-1))
        ref = Wb(yy(-1), x, pl.ds(0, 4), allr, cols(C))
        send("Cy2R", ref, ref, dy(1))
        recv("Cy1L", Wb(yy(1), x, allr, allr, cols(C)), dy(1))
        ref = Wb(yy(1), x, pl.ds(4, 4), allr, cols(C))
        send("Cy2L", ref, ref, dy(-1))

    def C3():
        recv("Cy2R", Wb(yy(2), x, pl.ds(0, 4), allr, cols(C)), dy(-1))
        recv("Cy2L", Wb(yy(2), x, pl.ds(4, 4), allr, cols(C)), dy(1))
        ref = Wb(allr, x, allr, allr, cols(C))
        send("Cx", ref, ref, dx)

    def C4():
        recv("Cx", Wb(allr, ox, allr, allr, cols(C)), dx)
        ref = Wb(allr, allr, allr, allr, cols(C))
        send("DC", ref, ref, dc)

    def grads(cr):
        def body(b, _):
            p = jnp.dot(ogT[b], hid2[:, cols(cr)], preferred_element_type=F32)
            G[b, :, :, :, cols(cr)] = p.reshape(NX, NZ, 16, cr[1])
            return 0

        lax.fori_loop(0, NY, body, 0)

    def RA1():
        def body(i, _):
            sa1[i] = G[i, :, zz(4), :, cols(A)].astype(BF)
            return 0

        lax.fori_loop(0, NY, body, 0)
        send("rA1R", sa1.at[pl.ds(0, 2)], ra1.at[0], dz(1))
        send("rA1L", sa1.at[pl.ds(2, 2)], ra1.at[1], dz(-1))

    def RA(step):
        d = 5 - step
        for side, o in ((0, d), (1, -d)):
            name = "RL"[side]
            zi = zz(o)
            dst = sa2.at[side, step - 2]
            if step == 2:
                recv(f"rA1{name}", ra1.at[side], dz(-1 if side == 0 else 1))
                base = 2 * side

                def with_recv(i, _):
                    dst[base + i] = (
                        G[base + i, :, zi, :, cols(A)] + ra1[side, i].astype(F32)
                    ).astype(BF)
                    return 0

                def without(i, _):
                    dst[2 - base + i] = G[2 - base + i, :, zi, :, cols(A)].astype(BF)
                    return 0

                lax.fori_loop(0, 2, without, 0)
                lax.fori_loop(0, 2, with_recv, 0)
            else:
                recv(f"rA{step - 1}{name}", ra2.at[side, step - 3], dz(-1 if side == 0 else 1))

                def full(i, _):
                    dst[i] = (
                        G[i, :, zi, :, cols(A)] + ra2[side, step - 3, i].astype(F32)
                    ).astype(BF)
                    return 0

                lax.fori_loop(0, NY, full, 0)
            send(f"rA{step}{name}", dst, ra2.at[side, step - 2], dz(1 if side == 0 else -1))

    def RA5():
        recv("rA4R", ra2.at[0, 2], dz(-1))
        recv("rA4L", ra2.at[1, 2], dz(1))

        def body(i, _):
            t = G[i, :, z, :, cols(A)] + ra2[0, 2, i].astype(F32) + ra2[1, 2, i].astype(F32)
            G[i, :, z, :, cols(A)] = t
            sa3[i] = t.astype(BF)
            return 0

        lax.fori_loop(0, NY, body, 0)
        for o in (2, 1, 3):
            send(f"rAy{o}", sa3.at[yy(o)], ra3.at[o - 1], dy(o))

    def RA6():
        for o in (1, 3, 2):
            recv(f"rAy{o}", ra3.at[o - 1], dy(-o))
        t = G[y, :, z, :, cols(A)]
        for o in (1, 2, 3):
            t = t + ra3[o - 1].astype(F32)
        G[y, :, z, :, cols(A)] = t
        sa4[...] = t.astype(BF)
        send("rAx", sa4.at[ox], ra4, dx)

    def RA7():
        recv("rAx", ra4, dx)
        fin[:, cols(A)] = G[y, x, z, :, cols(A)] + ra4[...].astype(F32)

    def RB1():
        def body(i, _):
            sb1[i] = G[yy(2), i, :, :, cols(B)].astype(BF)
            return 0

        lax.fori_loop(0, NX, body, 0)
        send("rB1R", sb1.at[0], rb1.at[0], dy(1))
        send("rB1L", sb1.at[1], rb1.at[1], dy(-1))

    def RB2():
        for side, o in ((0, 1), (1, -1)):
            name = "RL"[side]
            yi = yy(o)
            sb2[side, 1 - side] = G[yi, 1 - side, :, :, cols(B)].astype(BF)
            recv(f"rB1{name}", rb1.at[side], dy(-o))
            sb2[side, side] = (G[yi, side, :, :, cols(B)] + rb1[side].astype(F32)).astype(BF)
            send(f"rB2{name}", sb2.at[side], rb2.at[side], dy(o))

    def RB3():
        recv("rB2R", rb2.at[0], dy(-1))
        recv("rB2L", rb2.at[1], dy(1))
        sb3[...] = (
            G[y, ox, :, :, cols(B)] + rb2[0, ox].astype(F32) + rb2[1, ox].astype(F32)
        ).astype(BF)
        send("rBx", sb3, rb3, dx)
        G[y, x, :, :, cols(B)] = (
            G[y, x, :, :, cols(B)] + rb2[0, x].astype(F32) + rb2[1, x].astype(F32)
        )

    def RB4():
        recv("rBx", rb3, dx)
        t = G[y, x, :, :, cols(B)] + rb3[...].astype(F32)
        G[y, x, :, :, cols(B)] = t
        sb4[...] = t.astype(BF)
        for o in (4, 3, 5, 2, 6, 1, 7):
            send(f"rBz{o}", sb4.at[zz(o)], rb4.at[o - 1], dz(o))

    def RB5():
        t = G[y, x, z, :, cols(B)]
        for o in range(1, NZ):
            recv(f"rBz{o}", rb4.at[o - 1], dz(-o))
        for o in range(1, NZ):
            t = t + rb4[o - 1].astype(F32)
        fin[:, cols(B)] = t

    def RC1():
        def body(i, _):
            sc1[i] = G[i, ox, :, :, cols(C)].astype(BF)
            return 0

        lax.fori_loop(0, NY, body, 0)
        send("rCx", sc1, rc1, dx)

    def RC2():
        recv("rCx", rc1, dx)

        def body(i, _):
            G[i, x, :, :, cols(C)] = G[i, x, :, :, cols(C)] + rc1[i].astype(F32)
            return 0

        lax.fori_loop(0, NY, body, 0)
        sc2[...] = G[yy(2), x, :, :, cols(C)].astype(BF)
        send("rCy1R", sc2.at[pl.ds(0, 4)], rc2.at[0], dy(1))
        send("rCy1L", sc2.at[pl.ds(4, 4)], rc2.at[1], dy(-1))

    def RC3():
        for side, o in ((0, 1), (1, -1)):
            name = "RL"[side]
            yi = yy(o)
            w, n = 4 * side, 4 - 4 * side
            sc3[side, n : n + 4] = G[yi, x, n : n + 4, :, cols(C)].astype(BF)
            recv(f"rCy1{name}", rc2.at[side], dy(-o))
            sc3[side, w : w + 4] = (
                G[yi, x, w : w + 4, :, cols(C)] + rc2[side].astype(F32)
            ).astype(BF)
            send(f"rCy2{name}", sc3.at[side], rc3.at[side], dy(o))

    def RC4():
        recv("rCy2R", rc3.at[0], dy(-1))
        recv("rCy2L", rc3.at[1], dy(1))
        t = G[y, x, :, :, cols(C)] + rc3[0].astype(F32) + rc3[1].astype(F32)
        G[y, x, :, :, cols(C)] = t
        sc4[...] = t.astype(BF)
        for o in (4, 3, 5, 2, 6, 1, 7):
            send(f"rCz{o}", sc4.at[zz(o)], rc4.at[o - 1], dz(o))

    def RC5():
        t = G[y, x, z, :, cols(C)]
        for o in range(1, NZ):
            recv(f"rCz{o}", rc4.at[o - 1], dz(-o))
        for o in range(1, NZ):
            t = t + rc4[o - 1].astype(F32)
        fin[:, cols(C)] = t

    def forward(half, cr, hid, first):
        n = cr[1]
        w = W[half, :, :, :, :, cols(cr)].reshape(D, n)
        part = lax.dot_general(
            hid[0:TOK, cols(cr)], w, (((1,), (1,)), ((), ())), preferred_element_type=F32
        )
        if first:
            acc[...] = part
        else:
            acc[...] += part
        hg[:, 0:n] = jnp.dot(og_ref[...], w, preferred_element_type=F32)
        off = pl.multiple_of(half * HALF + cr[0], 128)

        def body(i, _):
            rows = pl.ds(pl.multiple_of(i * 16, 16), 16)
            g = gate_ref[rows, pl.ds(off, n)].astype(F32)
            u = up_ref[rows, pl.ds(off, n)].astype(F32)
            h = hg[rows, 0:n]
            s = jax.nn.sigmoid(g)
            gg_ref[rows, pl.ds(off, n)] = (h * u * s * (1.0 + g * (1.0 - s))).astype(BF)
            ug_ref[rows, pl.ds(off, n)] = (h * g * s).astype(BF)
            return 0

        lax.fori_loop(0, TOK // 16, body, 0)

    A1()
    recv("og", ogP, dc)
    for b in range(4):
        ogT[b, :, TOK : 2 * TOK] = ogP[:, b * 256 : (b + 1) * 256].T
    recv("h", hid2.at[pl.ds(TOK, TOK)], dc)
    grads(C)
    RC1()
    BC1()
    grads(B)
    RB1()
    A2()
    grads(A)
    RA1()
    B2()
    C2()
    A3(1)
    RB2()
    RA(2)
    C3()
    A3(2)
    B3()
    RA(3)
    RC2()
    A3(3)
    B4()
    RB3()
    RA(4)
    C4()
    RC3()
    A6()
    RB4()
    RA5()
    forward(c, B, hid2, True)
    RC4()
    RA6()
    forward(c, C, hid2, False)
    forward(c, A, hid2, False)
    RA7()
    recv("DB", W.at[oc, :, :, :, :, cols(B)], dc)
    forward(oc, B, hidO, False)
    recv("DC", W.at[oc, :, :, :, :, cols(C)], dc)
    forward(oc, C, hidO, False)
    recv("DA", W.at[oc, :, :, :, :, cols(A)], dc)
    forward(oc, A, hidO, False)
    lo_s[...] = acc[:, pl.ds(pl.multiple_of((1 - r) * 512, 128), 512)].astype(BF)
    send("lo", lo_s, lo_r, dr)
    RB5()
    RC5()
    send("fin", fin.at[pl.ds(pl.multiple_of(oc * 8, 8), 8)], finP, dc)

    def adam(half, g):
        cs = pl.ds(pl.multiple_of(half * HALF, 128), HALF)
        g = g / jnp.float32(32768)
        m = master_ref[:, cs]
        first = 0.9 * one_ref[:, cs] + 0.1 * g
        second = 0.95 * two_ref[:, cs] + 0.05 * g * g
        update = first / (1.0 - first_power) / (jnp.sqrt(second / (1.0 - second_power)) + 1e-08)
        master_out[:, cs] = m - 0.003 * (update + 0.1 * m)
        one_out[:, cs] = first
        two_out[:, cs] = second

    adam(c, fin[pl.ds(pl.multiple_of(c * 8, 8), 8), :])
    recv("fin", finP, dc)
    adam(oc, finP[...])
    recv("lo", lo_r, dr)
    out_ref[...] = (
        acc[:, pl.ds(pl.multiple_of(r * 512, 128), 512)] + lo_r[...].astype(F32)
    ).astype(BF)
    for d in sent:
        d.wait_send()
    assert len(slots) <= NSEM, len(slots)


NSEM = 80


def on_device(gate_pre, up_pre, out_grad, master, moment_one, moment_two):
    V = pltpu.VMEM
    nA, nB, nC = A[1], B[1], C[1]
    outs = pl.pallas_call(
        kernel,
        out_shape=(
            jax.ShapeDtypeStruct((TOK, 512), BF),
            jax.ShapeDtypeStruct((TOK, FF), BF),
            jax.ShapeDtypeStruct((TOK, FF), BF),
            jax.ShapeDtypeStruct((8, FF), F32),
            jax.ShapeDtypeStruct((8, FF), F32),
            jax.ShapeDtypeStruct((8, FF), F32),
        ),
        in_specs=[pl.BlockSpec(memory_space=V)] * 6,
        out_specs=[pl.BlockSpec(memory_space=V)] * 6,
        scratch_shapes=[
            V((NC, NY, NX, NZ, 16, HALF), BF),
            V((NY, NX, NZ, 16, HALF), F32),
            V((2 * TOK, HALF), BF),
            V((TOK, HALF), BF),
            V((TOK, D), BF),
            V((4, 256, 2 * TOK), BF),
            V((8, HALF), F32),
            V((TOK, 512), F32),
            V((TOK, D), F32),
            V((16, HALF), F32),
            V((8, HALF), F32),
            V((TOK, 512), BF),
            V((TOK, 512), BF),
            V((NY, NX, 16, nA), BF), V((2, 2, NX, 16, nA), BF),
            V((2, 3, NY, NX, 16, nA), BF), V((2, 3, NY, NX, 16, nA), BF),
            V((NY, NX, 16, nA), BF), V((3, NX, 16, nA), BF),
            V((NX, 16, nA), BF), V((16, nA), BF),
            V((NX, NZ, 16, nB), BF), V((2, NZ, 16, nB), BF),
            V((2, NX, NZ, 16, nB), BF), V((2, NX, NZ, 16, nB), BF),
            V((NZ, 16, nB), BF), V((NZ, 16, nB), BF),
            V((NZ, 16, nB), BF), V((7, 16, nB), BF),
            V((NY, NZ, 16, nC), BF), V((NY, NZ, 16, nC), BF),
            V((NZ, 16, nC), BF), V((2, 4, 16, nC), BF),
            V((2, NZ, 16, nC), BF), V((2, NZ, 16, nC), BF),
            V((NZ, 16, nC), BF), V((7, 16, nC), BF),
            pltpu.SemaphoreType.DMA((NSEM,)),
            pltpu.SemaphoreType.DMA((NSEM,)),
        ],
        compiler_params=pltpu.CompilerParams(
            collective_id=0, has_side_effects=True, vmem_limit_bytes=66_000_000
        ),
    )(
        gate_pre.reshape(TOK, FF),
        up_pre.reshape(TOK, FF),
        out_grad.reshape(TOK, D),
        master,
        moment_one,
        moment_two,
    )
    lo, gg, ug, mn, m1, m2 = outs
    return (
        lo.reshape(2, 128, 512),
        gg.reshape(2, 128, FF),
        ug.reshape(2, 128, FF),
        mn,
        m1,
        m2,
    )


def solution(mesh):
    torus = Mesh(
        mesh.devices.reshape(NY, NX, NZ, NC, mesh.shape["rep"]),
        ("dp_0", "dp_1", "dp_2", "dp_3", "rep"),
    )
    return jax.shard_map(
        on_device,
        mesh=torus,
        in_specs=(
            P(None, DP, "rep"),
            P(None, DP, "rep"),
            P(None, DP, None),
            P(DP, "rep"),
            P(DP, "rep"),
            P(DP, "rep"),
        ),
        out_specs=(
            P(None, DP, "rep"),
            P(None, DP, "rep"),
            P(None, DP, "rep"),
            P(DP, "rep"),
            P(DP, "rep"),
            P(DP, "rep"),
        ),
        check_vma=False,
    )
```

time: 642 us -> 80.2 us (0.12)
  the two profiles are of different devices: /device:TPU:1 before, /device:TPU:8 now
where the time goes in v1:
time: 80.2 us; the launch traced here: 80 us
  Pallas kernels  72 us (90%)
  local copies, waits for them, and re-layouts  7.37 us (9%)
    pallas_call x1, Pallas kernels, on_device(): pl.pallas_call(kernel, out_shape=(jax.ShapeDtypeStruct((TOK, 512), BF), j...  72 us
    unnamed x14, local copies, waits for them, and re-layouts  7.37 us

profile of v1, /device:TPU:8, one launch (start us, length us, event | category | flops | bytes accessed | tf_op | source)
XLA Modules:
  0.0 80.0 jit_solution(12773609934667879674)
XLA Ops:
  0.6 72.0 %shard_map.109 = (bf16[256,512]{1,0:T(8,128)(2,1)}, bf16[256,2816]{1,0:T(8,128)(2,1)}, bf16[256,2816]{1,0:T(8,128)(2,1)}, f32[8,2816]{1,0:T(8,128)}, f32[8,2816]{1,0:T(8,128)}, /*index=5*/f32[8,2816]{1,0:T(8,128)}) custom-call(bf16[256,2816]{1,0:T(8,128)(2,1)} %bitcast.6, bf16[256,2816]{1,0:T(8,128)(2,1)} %bitcast.7, bf16[256,1024]{1,0:T(8,128)(2,1)} %bitcast.10, ...), custom_call_target="tpu_custom_call" | custom-call | tf_op jit(solution)/shard_map/pallas_call | solution.py:493
  72.6 1.7 %copy.18 = bf16[2,128,512]{2,1,0:T(8,128)(2,1)} copy(bf16[2,128,512]{2,1,0:T(8,128)(2,1)} %bitcast.11) | data formatting | bytes 524288
  74.3 0.0 copy-start
  74.3 2.7 %copy.19 = bf16[2,128,2816]{2,1,0:T(8,128)(2,1)} copy(bf16[2,128,2816]{2,1,0:T(8,128)(2,1)} %bitcast.9) | data formatting | bytes 2883584
  77.0 0.0 copy-done
  77.0 0.0 copy-start.3
  77.0 0.0 copy-start.2
  77.0 0.0 copy-start.1
  77.0 1.1 %copy.20 = bf16[2,128,2816]{2,1,0:T(8,128)(2,1)} copy(bf16[2,128,2816]{2,1,0:T(8,128)(2,1)S(1)} %bitcast.8) | data formatting | bytes 2883584
  78.1 0.0 copy-done.3
  78.1 0.6 copy.21
  78.7 0.0 copy-done.2
  78.7 0.6 copy.22
  79.4 0.0 copy-done.1
  79.4 0.6 copy.23
Async XLA Ops:
  74.3 2.7 %copy-start = (bf16[256,2816]{1,0:T(8,128)(2,1)S(1)}, bf16[256,2816]{1,0:T(8,128)(2,1)}, u32[]{:S(2)}) copy-start(bf16[256,2816]{1,0:T(8,128)(2,1)} %get-tuple-element.14) | copy-start | bytes 4325380
  77.0 1.1 %copy-start.3 = (f32[8,2816]{1,0:T(8,128)S(1)}, f32[8,2816]{1,0:T(8,128)}, u32[]{:S(2)}) copy-start(f32[8,2816]{1,0:T(8,128)} %get-tuple-element.27) | copy-start | bytes 270340
  77.0 1.8 %copy-start.2 = (f32[8,2816]{1,0:T(8,128)S(1)}, f32[8,2816]{1,0:T(8,128)}, u32[]{:S(2)}) copy-start(f32[8,2816]{1,0:T(8,128)} %get-tuple-element.28) | copy-start | bytes 270340
  77.0 2.4 %copy-start.1 = (f32[8,2816]{1,0:T(8,128)S(1)}, f32[8,2816]{1,0:T(8,128)}, u32[]{:S(2)}) copy-start(f32[8,2816]{1,0:T(8,128)} %get-tuple-element.29) | copy-start | bytes 270340

commit v2 on v0

v2 whole, which is shorter than its diff:
```python
import jax
import jax.numpy as jnp
from jax import lax
from jax.experimental import pallas as pl
from jax.experimental.pallas import tpu as pltpu
from jax.sharding import Mesh
from jax.sharding import PartitionSpec as P

DP = ("dp_0", "dp_1", "dp_2", "dp_3")
NY, NX, NZ, NC = 4, 2, 8, 2

first_power = 2.6561398887587544e-05
second_power = 0.005920529220333997

F32 = jnp.float32
BF = jnp.bfloat16
D = 1024
FF = 2816
HALF = 1408
TOK = 256
A = (0, 512)
B = (512, 512)
C = (1024, 384)
BC = (512, 896)


def cols(r):
    return pl.ds(r[0], r[1])


class Names:
    def __getattr__(self, word):
        return word


K = Names()

ORDER = (
    K.init, K.A1, K.gp, K.gB, K.RB1, K.gC, K.RC1, K.gA, K.RA1, K.A2, K.RB2L, K.BC1, K.RC2,
    K.RA2R0, K.RA2L1, K.RA3R1, K.RA3L0, K.RC2b, K.RB2R, K.A3_1R0, K.A3_1L0, K.RC2c, K.C2R,
    K.A3_1R1, K.A3_1L1, K.RB3, K.RA3L1, K.RA3R0, K.B3R, K.RA4R1, K.RA4L0, K.RC3R, K.A3_2L0,
    K.A3_2R0, K.B2, K.C2L, K.A3_2R1, K.A3_2L1, K.RC3L, K.RA4L1, K.RA4R0, K.A3_3R0, K.B3L, K.C3,
    K.A3_3L1, K.RB4, K.RC4, K.RA5, K.A6, K.hg_cA, K.B4, K.lo_cB, K.C4, K.lo_cA, K.lo_cC,
    K.lo_oA, K.lo_oB, K.RA6, K.lo_oC, K.losend, K.hg_oB, K.hg_oC, K.hg_cB, K.RA7, K.RB5,
    K.hg_oA, K.hg_cC, K.RC5, K.fin_, K.adam, K.lofin,
)
ORDS = {
    K.init: (K.Zd7, K.Zd3, K.h, K.Zd6, K.Zd5, K.Zd1, K.Zd4, K.Zd2, K.Ax, K.og,),
    K.A1: (K.Ay2, K.Ay3, K.Ay1,),
    K.A2: (K.DA0, K.Az1L0, K.Az1R0, K.Az1R1, K.Az1L1,),
    K.A3_1R0: (K.Az2R0, K.DA1R0,),
    K.A3_1R1: (K.DA1R1, K.Az2R1,),
    K.A3_1L0: (K.Az2L0, K.DA1L0,),
    K.A3_1L1: (K.Az2L1, K.DA1L1,),
    K.A3_2R0: (K.DA2R0, K.Az3R0,),
    K.A3_2R1: (K.DA2R1, K.Az3R1,),
    K.A3_2L0: (K.DA2L0, K.Az3L0,),
    K.A3_2L1: (K.Az3L1, K.DA2L1,),
    K.A3_3R0: (K.Az4R0, K.DA3R0,),
    K.A3_3L1: (K.DA3L1, K.Az4L1,),
    K.BC1: (K.DB0, K.By1Lx, K.Cy1L, K.Bx, K.Cy1R, K.DC0, K.By1Rx, K.Cx0,),
    K.B2: (K.DB1, K.By1Ro, K.By1Lo,),
    K.B3R: (K.DB2, K.By2R,),
    K.B3L: (K.DB3, K.By2L,),
    K.C2R: (K.Cy2R, K.DC3, K.Cx3,),
    K.C2L: (K.DC1, K.Cx1, K.Cy2L,),
    K.C3: (K.Cx2, K.DC2,),
    K.RC1: (K.rCx2, K.rCx1, K.rCx3, K.rCx0,),
    K.RB1: (K.rB1L, K.rB2L1, K.rB2R1, K.rB1R,),
    K.RA1: (K.rA1L1, K.rA2L0, K.rA1R0, K.rA2R1,),
    K.RA5: (K.rAy2, K.rAy1, K.rAy3,),
    K.RB4: (K.rBz2, K.rBz7, K.rBz3, K.rBz6, K.rBz4, K.rBz1, K.rBz5,),
    K.RC2: (K.rCy1R, K.rCy1L,),
    K.RC4: (K.rCz7, K.rCz5, K.rCz4, K.rCz2, K.rCz3, K.rCz6, K.rCz1,),
}


def kernel(
    gate_hbm, up_hbm, og_hbm, master_hbm, one_hbm, two_hbm,
    out_hbm, gg_hbm, ug_hbm, master_out_hbm, one_out_hbm, two_out_hbm,
    gate_ref, up_ref, og_ref, master_ref, one_ref, two_ref,
    out_ref, gg_ref, ug_ref, master_out, one_out, two_out,
    W, G, hid2, hidO, ogP, ogT, mP, hg, acc, fin, finP, lo_s, lo_r,
    sa1, ra1, sa2, ra2, sa3, ra3, sa4, ra4,
    sb1, rb1, sb2, rb2, sb3, rb3, sb4, rb4,
    sc1, rc1, sc2, rc2, sc3, rc3, sc4, rc4,
    ssem, rsem, lsem,
):
    y = lax.axis_index(K.dp_0)
    x = lax.axis_index(K.dp_1)
    z = lax.axis_index(K.dp_2)
    c = lax.axis_index(K.dp_3)
    r = lax.axis_index(K.rep)
    oc = 1 - c
    ox = 1 - x

    def dy(o):
        return {K.dp_0: lax.rem(y + (o % NY), NY)}

    def dz(o):
        return {K.dp_2: lax.rem(z + (o % NZ), NZ)}

    def zz(o):
        return lax.rem(z + (o % NZ), NZ)

    def yy(o):
        return lax.rem(y + (o % NY), NY)

    dx = {K.dp_1: ox}
    dc = {K.dp_3: oc}
    dr = {K.rep: 1 - r}
    allr = slice(None)

    peers = [dc, dx, dr] + [dy(o) for o in range(1, NY)] + [dz(o) for o in range(1, NZ)]
    bar = pltpu.get_barrier_semaphore()
    for p in peers:
        pl.semaphore_signal(bar, inc=1, device_id=p, device_id_type=pl.DeviceIdType.MESH)

    loc = {}

    def local(name, src, dst):
        d = pltpu.make_async_copy(src, dst, lsem.at[len(loc)])
        d.start()
        loc[name] = d

    local(K.gate, gate_hbm, gate_ref)
    local(K.up, up_hbm, up_ref)
    local(K.og, og_hbm, og_ref)
    local(K.master, master_hbm, master_ref)
    local(K.one, one_hbm, one_ref)
    local(K.two, two_hbm, two_ref)

    sent = []
    slots = {}

    def slot(name):
        if name not in slots:
            slots[name] = len(slots)
        return slots[name]

    def rc(name, src, dst, dev):
        k = slot(name)
        return pltpu.make_async_remote_copy(
            src_ref=src, dst_ref=dst, send_sem=ssem.at[k], recv_sem=rsem.at[k],
            device_id=dev, device_id_type=pl.DeviceIdType.MESH,
        )

    def sends(step, items):
        names = ORDS.get(step, tuple(i[0] for i in items))
        table = {i[0]: i for i in items}
        for n in names:
            table[n]
        for name in list(names) + [n for n in table if n not in names]:
            _, src, dst, dev = table[name]
            d = rc(name, src, dst, dev)
            d.start()
            sent.append(d)

    def recv(name, dst, dev):
        with jax.named_scope(K.wait_ + name):
            rc(name, dst, dst, dev).wait_recv()

    def hidden_rows(half, out):
        off = pl.multiple_of(half * HALF, 128)

        def body(i, _):
            rows = pl.ds(pl.multiple_of(i * 16, 16), 16)
            g = gate_ref[rows, pl.ds(off, HALF)].astype(F32)
            u = up_ref[rows, pl.ds(off, HALF)].astype(F32)
            s = jax.nn.sigmoid(g)
            out[rows, :] = (g * s * u).astype(BF)
            return 0

        lax.fori_loop(0, TOK // 16, body, 0)

    def Wb(*idx):
        return W.at[(c,) + idx]

    def same(name, ref, dev):
        return (name, ref, ref, dev)

    S = {}

    def step(f):
        S[f.__name__] = f
        return f

    @step
    def init():
        sends(K.i0, [(K.m, master_ref.at[:, pl.ds(pl.multiple_of(oc * HALF, 128), HALF)], mP, dc)])
        recv(K.m, mP, dc)
        mine = master_ref[:, pl.ds(pl.multiple_of(c * HALF, 128), HALF)]
        theirs = mP[...]
        first_core = c == 0
        W[c, y, x, z] = jnp.concatenate(
            [jnp.where(first_core, mine, theirs), jnp.where(first_core, theirs, mine)], axis=0
        ).astype(BF)
        items = [
            (K.og, og_ref, ogP, dc),
            (K.h, hidO, hid2.at[pl.ds(TOK, TOK)], dc),
            same(K.Ax, Wb(y, x, z, allr, cols(A)), dx),
        ]
        for o in (4, 3, 5, 2, 6, 1, 7):
            items.append(same(f"Zd{o}", Wb(y, x, z, allr, cols(BC)), dz(o)))
        sends(K.init, items)

    @step
    def A1():
        recv(K.Ax, Wb(y, ox, z, allr, cols(A)), dx)
        ref = Wb(y, allr, z, allr, cols(A))
        sends(K.A1, [same(f"Ay{o}", ref, dy(o)) for o in (2, 1, 3)])

    def az(h, zi):
        return Wb(pl.ds(2 * h, 2), allr, zi, allr, cols(A))

    @step
    def A2():
        for o in (1, 3, 2):
            recv(f"Ay{o}", Wb(yy(-o), allr, z, allr, cols(A)), dy(-o))
        sends(K.A2, [
            same(K.Az1R0, az(0, z), dz(1)),
            same(K.Az1L1, az(1, z), dz(-1)),
            same(K.Az1R1, az(1, z), dz(1)),
            same(K.Az1L0, az(0, z), dz(-1)),
            same(K.DA0, Wb(allr, allr, z, allr, cols(A)), dc),
        ])

    def a3(s, sd, h):
        sg = 1 if sd == K.R else -1
        ref = az(h, zz(-sg * s))
        nm = f"{s}{sd}{h}"

        def f():
            recv(K.Az + nm, ref, dz(-sg))
            sends(K.A3_ + nm, [same(f"Az{s + 1}{sd}{h}", ref, dz(sg)), same(K.DA + nm, ref, dc)])

        S[K.A3_ + nm] = f

    last_a = (("3R1", 1, -3), ("3L0", 0, 3), ("4R0", 0, 4), ("4L1", 1, 4))
    for s in (1, 2, 3):
        for sd, h in ((K.R, 0), (K.L, 1), (K.R, 1), (K.L, 0)):
            if s < 3 or (sd == K.R) == (h == 0):
                a3(s, sd, h)

    @step
    def A6():
        for nm, h, o in last_a:
            recv(K.Az + nm, az(h, zz(o)), dz(-1 if K.R in nm else 1))
        sends(K.A6, [same(K.DA + nm, az(h, zz(o)), dc) for nm, h, o in last_a])

    def bref(yi, xi):
        return Wb(yi, xi, allr, allr, cols(B))

    def cref(yi, xi, zs=allr):
        return Wb(yi, xi, zs, allr, cols(C))

    @step
    def BC1():
        for o in (1, 7, 2, 6, 3, 5, 4):
            recv(f"Zd{o}", Wb(y, x, zz(-o), allr, cols(BC)), dz(-o))
        b, cc = bref(y, x), cref(y, x)
        sends(K.BC1, [
            same(K.Bx, b, dx), same(K.By1Rx, b, dy(1)), same(K.By1Lx, b, dy(-1)),
            same(K.Cy1R, cc, dy(1)), same(K.Cy1L, cc, dy(-1)), same(K.Cx0, cc, dx),
            same(K.DB0, b, dc), same(K.DC0, cc, dc),
        ])

    @step
    def B2():
        b = bref(y, ox)
        recv(K.Bx, b, dx)
        sends(K.B2, [same(K.By1Ro, b, dy(1)), same(K.By1Lo, b, dy(-1)), same(K.DB1, b, dc)])

    @step
    def B3R():
        b = bref(yy(-1), x)
        recv(K.By1Rx, b, dy(-1))
        sends(K.B3R, [same(K.By2R, b, dy(1)), same(K.DB2, b, dc)])

    @step
    def B3L():
        b = bref(yy(1), ox)
        recv(K.By1Lo, b, dy(1))
        sends(K.B3L, [same(K.By2L, b, dy(-1)), same(K.DB3, b, dc)])

    last_b = ((K.By2R, 2, x, -1), (K.By2L, 2, ox, 1), (K.By1Ro, -1, ox, -1), (K.By1Lx, 1, x, 1))

    @step
    def B4():
        for nm, o, xi, d in last_b:
            recv(nm, bref(yy(o), xi), dy(d))
        sends(K.B4, [same(K.D + nm, bref(yy(o), xi), dc) for nm, o, xi, d in last_b])

    lo4, hi4 = pl.ds(0, 4), pl.ds(4, 4)

    @step
    def C2R():
        recv(K.Cy1R, cref(yy(-1), x), dy(-1))
        sends(K.C2R, [
            same(K.Cy2R, cref(yy(-1), x, lo4), dy(1)),
            same(K.Cx3, cref(yy(-1), x), dx), same(K.DC3, cref(yy(-1), x), dc),
        ])

    @step
    def C2L():
        recv(K.Cy1L, cref(yy(1), x), dy(1))
        sends(K.C2L, [
            same(K.Cy2L, cref(yy(1), x, hi4), dy(-1)),
            same(K.Cx1, cref(yy(1), x), dx), same(K.DC1, cref(yy(1), x), dc),
        ])

    @step
    def C3():
        recv(K.Cy2R, cref(yy(2), x, lo4), dy(-1))
        recv(K.Cy2L, cref(yy(2), x, hi4), dy(1))
        sends(K.C3, [same(K.Cx2, cref(yy(2), x), dx), same(K.DC2, cref(yy(2), x), dc)])

    @step
    def C4():
        for o in (0, 1, 3, 2):
            recv(f"Cx{o}", cref(yy(o), ox), dx)
        sends(K.C4, [same(f"DCx{o}", cref(yy(o), ox), dc) for o in (0, 1, 3, 2)])

    @step
    def gp():
        recv(K.og, ogP, dc)
        for b in range(4):
            ogT[b, :, TOK : 2 * TOK] = ogP[:, b * 256 : (b + 1) * 256].T
        recv(K.h, hid2.at[pl.ds(TOK, TOK)], dc)

    def grads(cr):
        def body(b, _):
            p = jnp.dot(ogT[b], hid2[:, cols(cr)], preferred_element_type=F32)
            G[b, :, :, :, cols(cr)] = p.reshape(NX, NZ, 16, cr[1])
            return 0

        lax.fori_loop(0, NY, body, 0)

    S[K.gA] = lambda: grads(A)
    S[K.gB] = lambda: grads(B)
    S[K.gC] = lambda: grads(C)

    def ga(h, zi):
        return G[2 * h : 2 * h + 2, :, zi, :, cols(A)]

    @step
    def RA1():
        sa1[0] = ga(0, zz(4)).astype(BF)
        sa1[1] = ga(1, zz(4)).astype(BF)
        sa2[0, 0, 1] = ga(1, zz(3)).astype(BF)
        sa2[1, 0, 0] = ga(0, zz(-3)).astype(BF)
        sends(K.RA1, [
            (K.rA1R0, sa1.at[0], ra1.at[0], dz(1)),
            (K.rA1L1, sa1.at[1], ra1.at[1], dz(-1)),
            (K.rA2R1, sa2.at[0, 0, 1], ra2.at[0, 0, 1], dz(1)),
            (K.rA2L0, sa2.at[1, 0, 0], ra2.at[1, 0, 0], dz(-1)),
        ])

    def ra(s, sd, h):
        sg = 1 if sd == K.R else -1
        side = 0 if sd == K.R else 1

        def f():
            buf = ra1.at[side] if s == 2 else ra2.at[side, s - 3, h]
            recv(f"rA{s - 1}{sd}{h}", buf, dz(-sg))
            sa2[side, s - 2, h] = (ga(h, zz(sg * (5 - s))) + buf[...].astype(F32)).astype(BF)
            sends(K.RA, [(f"rA{s}{sd}{h}", sa2.at[side, s - 2, h], ra2.at[side, s - 2, h], dz(sg))])

        S[f"RA{s}{sd}{h}"] = f

    for sd in K.RL:
        for h in (0, 1):
            for s in range(2 if (sd == K.R) == (h == 0) else 3, 5):
                ra(s, sd, h)

    @step
    def RA5():
        for sd, d in ((K.R, -1), (K.L, 1)):
            for h in (0, 1):
                recv(f"rA4{sd}{h}", ra2.at[K.RL.index(sd), 2, h], dz(d))
        for h in (0, 1):
            t = ga(h, z) + ra2[0, 2, h].astype(F32) + ra2[1, 2, h].astype(F32)
            G[2 * h : 2 * h + 2, :, z, :, cols(A)] = t
            sa3[2 * h : 2 * h + 2] = t.astype(BF)
        sends(K.RA5, [(f"rAy{o}", sa3.at[yy(o)], ra3.at[o - 1], dy(o)) for o in (2, 1, 3)])

    @step
    def RA6():
        for o in (1, 3, 2):
            recv(f"rAy{o}", ra3.at[o - 1], dy(-o))
        t = G[y, :, z, :, cols(A)]
        for o in (1, 2, 3):
            t = t + ra3[o - 1].astype(F32)
        G[y, :, z, :, cols(A)] = t
        sa4[...] = t.astype(BF)
        sends(K.RA6, [(K.rAx, sa4.at[ox], ra4, dx)])

    @step
    def RA7():
        recv(K.rAx, ra4, dx)
        fin[:, cols(A)] = G[y, x, z, :, cols(A)] + ra4[...].astype(F32)

    def gb(yi, xi):
        return G[yi, xi, :, :, cols(B)]

    @step
    def RB1():
        sb1[0] = gb(yy(2), x).astype(BF)
        sb1[1] = gb(yy(2), ox).astype(BF)
        sb2[0, 1] = gb(yy(1), ox).astype(BF)
        sb2[1, 0] = gb(yy(-1), x).astype(BF)
        sends(K.RB1, [
            (K.rB1R, sb1.at[0], rb1.at[0], dy(1)), (K.rB1L, sb1.at[1], rb1.at[1], dy(-1)),
            (K.rB2R1, sb2.at[0, 1], rb2.at[0, 1], dy(1)),
            (K.rB2L1, sb2.at[1, 0], rb2.at[1, 0], dy(-1)),
        ])

    @step
    def RB2R():
        recv(K.rB1R, rb1.at[0], dy(-1))
        sb2[0, 0] = (gb(yy(1), x) + rb1[0].astype(F32)).astype(BF)
        sends(K.RB2R, [(K.rB2R0, sb2.at[0, 0], rb2.at[0, 0], dy(1))])

    @step
    def RB2L():
        recv(K.rB1L, rb1.at[1], dy(1))
        sb2[1, 1] = (gb(yy(-1), ox) + rb1[1].astype(F32)).astype(BF)
        sends(K.RB2L, [(K.rB2L0, sb2.at[1, 1], rb2.at[1, 1], dy(-1))])

    @step
    def RB3():
        recv(K.rB2R1, rb2.at[0, 1], dy(-1))
        recv(K.rB2L0, rb2.at[1, 1], dy(1))
        sb3[...] = (gb(y, ox) + rb2[0, 1].astype(F32) + rb2[1, 1].astype(F32)).astype(BF)
        sends(K.RB3, [(K.rBx, sb3, rb3, dx)])

    @step
    def RB4():
        recv(K.rB2R0, rb2.at[0, 0], dy(-1))
        recv(K.rB2L1, rb2.at[1, 0], dy(1))
        recv(K.rBx, rb3, dx)
        t = gb(y, x) + rb2[0, 0].astype(F32) + rb2[1, 0].astype(F32) + rb3[...].astype(F32)
        G[y, x, :, :, cols(B)] = t
        sb4[...] = t.astype(BF)
        sends(K.RB4, [(f"rBz{o}", sb4.at[zz(o)], rb4.at[o - 1], dz(o)) for o in (4, 3, 5, 2, 6, 1, 7)])

    @step
    def RB5():
        t = G[y, x, z, :, cols(B)]
        for o in range(1, NZ):
            recv(f"rBz{o}", rb4.at[o - 1], dz(-o))
        for o in range(1, NZ):
            t = t + rb4[o - 1].astype(F32)
        fin[:, cols(B)] = t

    def gc(yi, xi, zs=allr):
        return G[yi, xi, zs, :, cols(C)]

    @step
    def RC1():
        items = []
        for o in (2, 1, 3, 0):
            sc1[o] = gc(yy(o), ox).astype(BF)
            items.append((f"rCx{o}", sc1.at[o], rc1.at[o], dx))
        sends(K.RC1, items)

    @step
    def RC2():
        recv(K.rCx2, rc1.at[2], dx)
        sc2[...] = (gc(yy(2), x) + rc1[2].astype(F32)).astype(BF)
        sends(K.RC2, [
            (K.rCy1R, sc2.at[lo4], rc2.at[0], dy(1)), (K.rCy1L, sc2.at[hi4], rc2.at[1], dy(-1)),
        ])

    @step
    def RC2b():
        recv(K.rCx1, rc1.at[1], dx)
        t = gc(yy(1), x) + rc1[1].astype(F32)
        G[yy(1), x, :, :, cols(C)] = t
        sc3[0, 4:8] = t[4:8].astype(BF)
        sends(K.RC2b, [(K.rCy2R1, sc3.at[0, hi4], rc3.at[0, hi4], dy(1))])

    @step
    def RC2c():
        recv(K.rCx3, rc1.at[3], dx)
        t = gc(yy(3), x) + rc1[3].astype(F32)
        G[yy(3), x, :, :, cols(C)] = t
        sc3[1, 0:4] = t[0:4].astype(BF)
        sends(K.RC2c, [(K.rCy2L1, sc3.at[1, lo4], rc3.at[1, lo4], dy(-1))])

    @step
    def RC3R():
        recv(K.rCy1R, rc2.at[0], dy(-1))
        sc3[0, 0:4] = (gc(yy(1), x, slice(0, 4)) + rc2[0].astype(F32)).astype(BF)
        sends(K.RC3R, [(K.rCy2R0, sc3.at[0, lo4], rc3.at[0, lo4], dy(1))])

    @step
    def RC3L():
        recv(K.rCy1L, rc2.at[1], dy(1))
        sc3[1, 4:8] = (gc(yy(3), x, slice(4, 8)) + rc2[1].astype(F32)).astype(BF)
        sends(K.RC3L, [(K.rCy2L0, sc3.at[1, hi4], rc3.at[1, hi4], dy(-1))])

    @step
    def RC4():
        recv(K.rCx0, rc1.at[0], dx)
        recv(K.rCy2R0, rc3.at[0, lo4], dy(-1))
        recv(K.rCy2R1, rc3.at[0, hi4], dy(-1))
        recv(K.rCy2L0, rc3.at[1, hi4], dy(1))
        recv(K.rCy2L1, rc3.at[1, lo4], dy(1))
        t = gc(y, x) + rc1[0].astype(F32) + rc3[0].astype(F32) + rc3[1].astype(F32)
        G[y, x, :, :, cols(C)] = t
        sc4[...] = t.astype(BF)
        sends(K.RC4, [(f"rCz{o}", sc4.at[zz(o)], rc4.at[o - 1], dz(o)) for o in (4, 3, 5, 2, 6, 1, 7)])

    @step
    def RC5():
        t = G[y, x, z, :, cols(C)]
        for o in range(1, NZ):
            recv(f"rCz{o}", rc4.at[o - 1], dz(-o))
        for o in range(1, NZ):
            t = t + rc4[o - 1].astype(F32)
        fin[:, cols(C)] = t

    def partner_pieces(k):
        if k == K.A:
            yield K.DA0, W.at[oc, :, :, z, :, cols(A)]
            for s in (1, 2, 3, 4):
                for sd, sg in ((K.R, 1), (K.L, -1)):
                    for h in (0, 1):
                        if s < 4 or (sd == K.R) == (h == 0):
                            yield f"DA{s}{sd}{h}", W.at[oc, pl.ds(2 * h, 2), :, zz(-sg * s), :, cols(A)]
        if k == K.B:
            for nm, o, xi in (
                (K.DB0, 0, x), (K.DB1, 0, ox), (K.DB2, -1, x), (K.DB3, 1, ox),
                (K.DBy1Ro, -1, ox), (K.DBy1Lx, 1, x), (K.DBy2R, 2, x), (K.DBy2L, 2, ox),
            ):
                yield nm, W.at[oc, yy(o), xi, :, :, cols(B)]
        if k == K.C:
            for o in (0, 1, 3, 2):
                yield f"DC{o}", W.at[oc, yy(o), x, :, :, cols(C)]
                yield f"DCx{o}", W.at[oc, yy(o), ox, :, :, cols(C)]

    ranges = {K.A: A, K.B: B, K.C: C}
    have = set()
    started = []

    def w_of(side, k):
        if side == K.o and k not in have:
            have.add(k)
            for nm, ref in partner_pieces(k):
                recv(nm, ref, dc)
        half = c if side == K.c else oc
        return W[half, :, :, :, :, cols(ranges[k])].reshape(D, ranges[k][1])

    def lo(side, k):
        w = w_of(side, k)
        h = (hid2 if side == K.c else hidO)[0:TOK, cols(ranges[k])]
        part = lax.dot_general(h, w, (((1,), (1,)), ((), ())), preferred_element_type=F32)
        if started:
            acc[...] += part
        else:
            acc[...] = part
        started.append(1)

    def hgrad(side, k):
        n = ranges[k][1]
        half = c if side == K.c else oc
        hg[:, 0:n] = jnp.dot(og_ref[...], w_of(side, k), preferred_element_type=F32)
        cs = pl.ds(pl.multiple_of(half * HALF + ranges[k][0], 128), n)

        def body(i, _):
            rows = pl.ds(pl.multiple_of(i * 16, 16), 16)
            g = gate_ref[rows, cs].astype(F32)
            u = up_ref[rows, cs].astype(F32)
            h = hg[rows, 0:n]
            s = jax.nn.sigmoid(g)
            gg_ref[rows, cs] = (h * u * s * (1.0 + g * (1.0 - s))).astype(BF)
            ug_ref[rows, cs] = (h * g * s).astype(BF)
            return 0

        lax.fori_loop(0, TOK // 16, body, 0)
        local(f"gg{side}{k}", gg_ref.at[:, cs], gg_hbm.at[:, cs])
        local(f"ug{side}{k}", ug_ref.at[:, cs], ug_hbm.at[:, cs])

    for side in K.co:
        for k in K.ABC:
            S[f"lo_{side}{k}"] = lambda side=side, k=k: lo(side, k)
            S[f"hg_{side}{k}"] = lambda side=side, k=k: hgrad(side, k)

    @step
    def losend():
        lo_s[...] = acc[:, pl.ds(pl.multiple_of((1 - r) * 512, 128), 512)].astype(BF)
        sends(K.losend, [(K.lo, lo_s, lo_r, dr)])

    @step
    def lofin():
        recv(K.lo, lo_r, dr)
        out_ref[...] = (
            acc[:, pl.ds(pl.multiple_of(r * 512, 128), 512)] + lo_r[...].astype(F32)
        ).astype(BF)
        local(K.out, out_ref, out_hbm)

    def update(half, g):
        cs = pl.ds(pl.multiple_of(half * HALF, 128), HALF)
        g = g / jnp.float32(32768)
        m = master_ref[:, cs]
        first = 0.9 * one_ref[:, cs] + 0.1 * g
        second = 0.95 * two_ref[:, cs] + 0.05 * g * g
        upd = first / (1.0 - first_power) / (jnp.sqrt(second / (1.0 - second_power)) + 1e-08)
        master_out[:, cs] = m - 0.003 * (upd + 0.1 * m)
        one_out[:, cs] = first
        two_out[:, cs] = second

    @step
    def fin_():
        sends(K.fin, [(K.fin, fin.at[pl.ds(pl.multiple_of(oc * 8, 8), 8)], finP, dc)])
        update(c, fin[pl.ds(pl.multiple_of(c * 8, 8), 8), :])

    @step
    def adam():
        recv(K.fin, finP, dc)
        update(oc, finP[...])
        local(K.mo, master_out, master_out_hbm)
        local(K.oo, one_out, one_out_hbm)
        local(K.to, two_out, two_out_hbm)

    with jax.named_scope(K.loads):
        loc[K.gate].wait()
        loc[K.up].wait()
    with jax.named_scope(K.hidden):
        hidden_rows(oc, hidO)
        hidden_rows(c, hid2)
    for n in (K.og, K.master, K.one, K.two):
        loc[n].wait()
    with jax.named_scope(K.transpose):
        for b in range(4):
            ogT[b, :, 0:TOK] = og_ref[:, b * 256 : (b + 1) * 256].T
    with jax.named_scope(K.barrier):
        pl.semaphore_wait(bar, len(peers))
    for n in ORDER:
        with jax.named_scope(n):
            S.pop(n)()
    assert not S, S.keys()
    with jax.named_scope(K.sends_done):
        for d in sent:
            d.wait_send()
        for n, d in loc.items():
            if n not in (K.gate, K.up, K.og, K.master, K.one, K.two):
                d.wait()
    assert len(slots) <= NSEM, len(slots)


NSEM = 144


def copy_kernel(*refs):
    src, dst, buf, sem = refs[0:6], refs[6:12], refs[12:18], refs[18]
    parts = []
    for i in (1, 2, 0, 3, 4, 5):
        rows = src[i].shape[0]
        n = 2 if rows > 8 else 1
        for j in range(n):
            rs = pl.ds(j * (rows // n), rows // n)
            k = len(parts)
            parts.append((
                pltpu.make_async_copy(src[i].at[rs], buf[i].at[rs], sem.at[0, k]),
                pltpu.make_async_copy(buf[i].at[rs], dst[i].at[rs], sem.at[1, k]),
            ))
    for a, _ in parts:
        a.start()
    for a, b in parts:
        a.wait()
        b.start()
    for _, b in parts:
        b.wait()


def on_device(gate_pre, up_pre, out_grad, master, moment_one, moment_two):
    V = pltpu.VMEM
    nA, nB, nC = A[1], B[1], C[1]
    outs = pl.pallas_call(
        kernel,
        out_shape=(
            jax.ShapeDtypeStruct((TOK, 512), BF),
            jax.ShapeDtypeStruct((TOK, FF), BF),
            jax.ShapeDtypeStruct((TOK, FF), BF),
            jax.ShapeDtypeStruct((8, FF), F32),
            jax.ShapeDtypeStruct((8, FF), F32),
            jax.ShapeDtypeStruct((8, FF), F32),
        ),
        in_specs=[pl.BlockSpec(memory_space=pl.ANY)] * 6,
        out_specs=[pl.BlockSpec(memory_space=pl.ANY)] * 6,
        scratch_shapes=[
            V((TOK, FF), BF), V((TOK, FF), BF), V((TOK, D), BF),
            V((8, FF), F32), V((8, FF), F32), V((8, FF), F32),
            V((TOK, 512), BF), V((TOK, FF), BF), V((TOK, FF), BF),
            V((8, FF), F32), V((8, FF), F32), V((8, FF), F32),
            V((NC, NY, NX, NZ, 16, HALF), BF),
            V((NY, NX, NZ, 16, HALF), F32),
            V((2 * TOK, HALF), BF),
            V((TOK, HALF), BF),
            V((TOK, D), BF),
            V((4, 256, 2 * TOK), BF),
            V((8, HALF), F32),
            V((TOK, 512), F32),
            V((TOK, D), F32),
            V((16, HALF), F32),
            V((8, HALF), F32),
            V((TOK, 512), BF),
            V((TOK, 512), BF),
            V((2, 2, NX, 16, nA), BF), V((2, 2, NX, 16, nA), BF),
            V((2, 3, 2, 2, NX, 16, nA), BF), V((2, 3, 2, 2, NX, 16, nA), BF),
            V((NY, NX, 16, nA), BF), V((3, NX, 16, nA), BF),
            V((NX, 16, nA), BF), V((16, nA), BF),
            V((NX, NZ, 16, nB), BF), V((2, NZ, 16, nB), BF),
            V((2, NX, NZ, 16, nB), BF), V((2, NX, NZ, 16, nB), BF),
            V((NZ, 16, nB), BF), V((NZ, 16, nB), BF),
            V((NZ, 16, nB), BF), V((7, 16, nB), BF),
            V((NY, NZ, 16, nC), BF), V((NY, NZ, 16, nC), BF),
            V((NZ, 16, nC), BF), V((2, 4, 16, nC), BF),
            V((2, NZ, 16, nC), BF), V((2, NZ, 16, nC), BF),
            V((NZ, 16, nC), BF), V((7, 16, nC), BF),
            pltpu.SemaphoreType.DMA((NSEM,)),
            pltpu.SemaphoreType.DMA((NSEM,)),
            pltpu.SemaphoreType.DMA((24,)),
        ],
        compiler_params=pltpu.CompilerParams(
            collective_id=0, has_side_effects=True, vmem_limit_bytes=66_000_000
        ),
    )(
        gate_pre.reshape(TOK, FF),
        up_pre.reshape(TOK, FF),
        out_grad.reshape(TOK, D),
        master,
        moment_one,
        moment_two,
    )
    outs = pl.pallas_call(
        copy_kernel,
        out_shape=tuple(jax.ShapeDtypeStruct(o.shape, o.dtype) for o in outs),
        in_specs=[pl.BlockSpec(memory_space=pl.ANY)] * 6,
        out_specs=[pl.BlockSpec(memory_space=pl.ANY)] * 6,
        scratch_shapes=[V(o.shape, o.dtype) for o in outs] + [pltpu.SemaphoreType.DMA((2, 12))],
    )(*outs)
    lo, gg, ug, mn, m1, m2 = outs
    return (
        lo.reshape(2, 128, 512),
        gg.reshape(2, 128, FF),
        ug.reshape(2, 128, FF),
        mn,
        m1,
        m2,
    )


def solution(mesh):
    torus = Mesh(
        mesh.devices.reshape(NY, NX, NZ, NC, mesh.shape["rep"]),
        ("dp_0", "dp_1", "dp_2", "dp_3", "rep"),
    )
    return jax.shard_map(
        on_device,
        mesh=torus,
        in_specs=(
            P(None, DP, "rep"),
            P(None, DP, "rep"),
            P(None, DP, None),
            P(DP, "rep"),
            P(DP, "rep"),
            P(DP, "rep"),
        ),
        out_specs=(
            P(None, DP, "rep"),
            P(None, DP, "rep"),
            P(None, DP, "rep"),
            P(DP, "rep"),
            P(DP, "rep"),
            P(DP, "rep"),
        ),
        check_vma=False,
    )
```

time: 642 us -> 60.6 us (0.09)
  waiting for transfers between devices: 576 us -> 0 us
  Pallas kernels: 0 us -> 59.4 us
  matrix products: 24.3 us -> 0 us
  between operations: 13.8 us -> 0.64 us
  local copies, waits for them, and re-layouts: 10.2 us -> 0 us
  starting transfers between devices: 8.49 us -> 0 us
    reduce_scatter x2 -> x0, waiting for transfers between devices: 314 us -> none  [the longest x1 284 us: sum_by_chip_2(): return lax.psum_scatter(parts, chips, scatter_dimension=0, tiled=True)[0]]
    all_gather x1 -> x0, waiting for transfers between devices: 259 us -> none  [on_device(): weights = lax.all_gather(shard_bf, DP, axis=0, tiled=True)]
    pallas_call x0 -> x2, Pallas kernels: none -> 59.4 us  [the longest x1 56.4 us: on_device(): pl.pallas_call(kernel, out_shape=(jax.ShapeDtypeStruct((TOK, 512), BF), j...]
    dot_general x6 -> x0, matrix products: 24.3 us -> none  [the longest x2 9.25 us: grad_rows(): lax.dot_general(cotangent, hidden, (((0,), (0,)), ((), ())), preferred_el...]
    add x1 -> x0, local copies, waits for them, and re-layouts: 9.49 us -> none  [on_device(): grad_sum = shard_grad if grad_sum is None else grad_sum + shard_grad]
    all_to_all x2 -> x0, starting transfers between devices: 8.37 us -> none  [sent_and_summed(): parts = lax.all_to_all(in_blocks(x, dim, peers), axis, 0, 0, tiled=True)]
  transfers between devices with their start and end apart: 5 -> 0, of which waited for: 4 -> 0; matrix products, arithmetic and copies ran while one was open for 2% -> 0% of each run, Pallas kernels for 0% -> 0%
where the time goes in v2:
time: 60.6 us; the launch traced here: 60.1 us
  Pallas kernels  59.4 us (98%)
  between operations  0.64 us (1%)
    pallas_call x1, Pallas kernels, on_device(): pl.pallas_call(kernel, out_shape=(jax.ShapeDtypeStruct((TOK, 512), BF), j...  56.4 us
    pallas_call x1, Pallas kernels, on_device(): pl.pallas_call(copy_kernel, out_shape=tuple((jax.ShapeDtypeStruct(o.shape...  3.06 us

profile of v2, /device:TPU:1, one launch (start us, length us, event | category | flops | bytes accessed | tf_op | source)
XLA Modules:
  0.0 60.1 jit_solution(13980919827008233259)
XLA Ops:
  0.6 56.4 %shard_map.109 = (bf16[256,512]{1,0:T(8,128)(2,1)}, bf16[256,2816]{1,0:T(8,128)(2,1)}, bf16[256,2816]{1,0:T(8,128)(2,1)}, f32[8,2816]{1,0:T(8,128)}, f32[8,2816]{1,0:T(8,128)}, /*index=5*/f32[8,2816]{1,0:T(8,128)}) custom-call(bf16[256,2816]{1,0:T(8,128)(2,1)} %bitcast.6, bf16[256,2816]{1,0:T(8,128)(2,1)} %bitcast.7, bf16[256,1024]{1,0:T(8,128)(2,1)} %bitcast.8, ...), custom_call_target="tpu_custom_call" | custom-call | tf_op jit(solution)/shard_map/pallas_call | solution.py:681
  57.0 3.1 %shard_map.110 = (bf16[256,512]{1,0:T(8,128)(2,1)}, bf16[256,2816]{1,0:T(8,128)(2,1)}, bf16[256,2816]{1,0:T(8,128)(2,1)}, f32[8,2816]{1,0:T(8,128)}, f32[8,2816]{1,0:T(8,128)}, /*index=5*/f32[8,2816]{1,0:T(8,128)}) custom-call(bf16[256,512]{1,0:T(8,128)(2,1)} %get-tuple-element.18.refs_0_, bf16[256,2816]{1,0:T(8,128)(2,1)} %get-tuple-element.19.refs_1_, ...), custom_call_target="tpu_custom_call" | custom-call | tf_op jit(solution)/shard_map/pallas_call | solution.py:738

commit v3 on v2

--- a/solution.py
+++ b/solution.py
@@ -36,50 +36,49 @@
 K = Names()
 
 ORDER = (
-    K.init, K.A1, K.gp, K.gB, K.RB1, K.gC, K.RC1, K.gA, K.RA1, K.A2, K.RB2L, K.BC1, K.RC2,
-    K.RA2R0, K.RA2L1, K.RA3R1, K.RA3L0, K.RC2b, K.RB2R, K.A3_1R0, K.A3_1L0, K.RC2c, K.C2R,
-    K.A3_1R1, K.A3_1L1, K.RB3, K.RA3L1, K.RA3R0, K.B3R, K.RA4R1, K.RA4L0, K.RC3R, K.A3_2L0,
-    K.A3_2R0, K.B2, K.C2L, K.A3_2R1, K.A3_2L1, K.RC3L, K.RA4L1, K.RA4R0, K.A3_3R0, K.B3L, K.C3,
-    K.A3_3L1, K.RB4, K.RC4, K.RA5, K.A6, K.hg_cA, K.B4, K.lo_cB, K.C4, K.lo_cA, K.lo_cC,
-    K.lo_oA, K.lo_oB, K.RA6, K.lo_oC, K.losend, K.hg_oB, K.hg_oC, K.hg_cB, K.RA7, K.RB5,
-    K.hg_oA, K.hg_cC, K.RC5, K.fin_, K.adam, K.lofin,
+    K.init, K.hidO_, K.A1, K.hid2_, K.gp, K.gB, K.RB1, K.gC, K.RC1, K.A2, K.gA, K.RA1, K.A3_1L1,
+    K.RB2L, K.A3_1L0, K.A3_1R1, K.BC1, K.RA3R1, K.RA2L0, K.A3_1R0, K.A3_2R1, K.A3_2L1, K.C2R,
+    K.A3_2L0, K.C2L, K.RB2R, K.RA4R1, K.A3_2R0, K.B2, K.A3_3L1, K.C3, K.RC2, K.A3_3L0, K.RA3R0,
+    K.RA2L1, K.RA3L0, K.B3R, K.B3L, K.RC2b, K.RC2c, K.A6, K.RB3, K.RA4R0, K.RA3L1, K.RA4L0,
+    K.C4, K.lo_cC, K.lo_oA, K.B4, K.RA4L1, K.lo_cB, K.lo_oC, K.lo_cA, K.RB4, K.lo_oB, K.losend,
+    K.RC3L, K.RC3R, K.hg_cB, K.RA5, K.hg_oA, K.RC4, K.hg_cA, K.hg_oC, K.hg_oB, K.RA6, K.hg_cC,
+    K.RB5, K.RC5, K.RA7, K.fin_, K.lofin, K.adam,
 )
 ORDS = {
-    K.init: (K.Zd7, K.Zd3, K.h, K.Zd6, K.Zd5, K.Zd1, K.Zd4, K.Zd2, K.Ax, K.og,),
-    K.A1: (K.Ay2, K.Ay3, K.Ay1,),
-    K.A2: (K.DA0, K.Az1L0, K.Az1R0, K.Az1R1, K.Az1L1,),
-    K.A3_1R0: (K.Az2R0, K.DA1R0,),
-    K.A3_1R1: (K.DA1R1, K.Az2R1,),
+    K.init: (K.Zd2, K.Zd6, K.Zd3, K.Zd4, K.og, K.Zd1, K.Zd7, K.Zd5, K.Ax,),
+    K.A1: (K.Ay2, K.Ay1, K.Ay3,),
+    K.A2: (K.Az1L1, K.DA0, K.Az1L0, K.Az1R1, K.Az1R0,),
+    K.A3_1R0: (K.DA1R0, K.Az2R0,),
+    K.A3_1R1: (K.Az2R1, K.DA1R1,),
     K.A3_1L0: (K.Az2L0, K.DA1L0,),
-    K.A3_1L1: (K.Az2L1, K.DA1L1,),
+    K.A3_1L1: (K.DA1L1, K.Az2L1,),
     K.A3_2R0: (K.DA2R0, K.Az3R0,),
-    K.A3_2R1: (K.DA2R1, K.Az3R1,),
-    K.A3_2L0: (K.DA2L0, K.Az3L0,),
+    K.A3_2R1: (K.Az3R1, K.DA2R1,),
+    K.A3_2L0: (K.Az3L0, K.DA2L0,),
     K.A3_2L1: (K.Az3L1, K.DA2L1,),
-    K.A3_3R0: (K.Az4R0, K.DA3R0,),
+    K.A3_3L0: (K.Az4L0, K.DA3L0,),
     K.A3_3L1: (K.DA3L1, K.Az4L1,),
-    K.BC1: (K.DB0, K.By1Lx, K.Cy1L, K.Bx, K.Cy1R, K.DC0, K.By1Rx, K.Cx0,),
-    K.B2: (K.DB1, K.By1Ro, K.By1Lo,),
+    K.BC1: (K.Cy1L, K.Cy1R, K.Bx, K.DB0, K.Cx0, K.By1Rx, K.DC0, K.By1Lx,),
+    K.B2: (K.By1Ro, K.DB1, K.By1Lo,),
     K.B3R: (K.DB2, K.By2R,),
     K.B3L: (K.DB3, K.By2L,),
-    K.C2R: (K.Cy2R, K.DC3, K.Cx3,),
-    K.C2L: (K.DC1, K.Cx1, K.Cy2L,),
+    K.C2R: (K.DC3, K.Cy2R, K.Cx3,),
+    K.C2L: (K.Cx1, K.Cy2L, K.DC1,),
     K.C3: (K.Cx2, K.DC2,),
-    K.RC1: (K.rCx2, K.rCx1, K.rCx3, K.rCx0,),
-    K.RB1: (K.rB1L, K.rB2L1, K.rB2R1, K.rB1R,),
-    K.RA1: (K.rA1L1, K.rA2L0, K.rA1R0, K.rA2R1,),
-    K.RA5: (K.rAy2, K.rAy1, K.rAy3,),
-    K.RB4: (K.rBz2, K.rBz7, K.rBz3, K.rBz6, K.rBz4, K.rBz1, K.rBz5,),
+    K.RC1: (K.rCx3, K.rCx2, K.rCx0, K.rCx1,),
+    K.RB1: (K.rB1R, K.rB1L, K.rB2L1, K.rB2R1,),
+    K.RA1: (K.rA2R1, K.rA1L1, K.rA2R0, K.rA1L0,),
+    K.RA5: (K.rAy3, K.rAy1, K.rAy2,),
+    K.RB4: (K.rBz7, K.rBz1, K.rBz4, K.rBz2, K.rBz6, K.rBz5, K.rBz3,),
     K.RC2: (K.rCy1R, K.rCy1L,),
-    K.RC4: (K.rCz7, K.rCz5, K.rCz4, K.rCz2, K.rCz3, K.rCz6, K.rCz1,),
+    K.RC4: (K.rCz4, K.rCz5, K.rCz3, K.rCz2, K.rCz6, K.rCz1, K.rCz7,),
 }
 
 
 def kernel(
     gate_hbm, up_hbm, og_hbm, master_hbm, one_hbm, two_hbm,
-    out_hbm, gg_hbm, ug_hbm, master_out_hbm, one_out_hbm, two_out_hbm,
+    out_ref, gg_ref, ug_ref, master_out, one_out, two_out,
     gate_ref, up_ref, og_ref, master_ref, one_ref, two_ref,
-    out_ref, gg_ref, ug_ref, master_out, one_out, two_out,
     W, G, hid2, hidO, ogP, ogT, mP, hg, acc, fin, finP, lo_s, lo_r,
     sa1, ra1, sa2, ra2, sa3, ra3, sa4, ra4,
     sb1, rb1, sb2, rb2, sb3, rb3, sb4, rb4,
@@ -123,10 +122,10 @@
         d.start()
         loc[name] = d
 
+    local(K.master, master_hbm, master_ref)
+    local(K.og, og_hbm, og_ref)
     local(K.gate, gate_hbm, gate_ref)
     local(K.up, up_hbm, up_ref)
-    local(K.og, og_hbm, og_ref)
-    local(K.master, master_hbm, master_ref)
     local(K.one, one_hbm, one_ref)
     local(K.two, two_hbm, two_ref)
 
@@ -195,9 +194,9 @@
         W[c, y, x, z] = jnp.concatenate(
             [jnp.where(first_core, mine, theirs), jnp.where(first_core, theirs, mine)], axis=0
         ).astype(BF)
+        loc[K.og].wait()
         items = [
             (K.og, og_ref, ogP, dc),
-            (K.h, hidO, hid2.at[pl.ds(TOK, TOK)], dc),
             same(K.Ax, Wb(y, x, z, allr, cols(A)), dx),
         ]
         for o in (4, 3, 5, 2, 6, 1, 7):
@@ -205,6 +204,19 @@
         sends(K.init, items)
 
     @step
+    def hidO_():
+        loc[K.gate].wait()
+        loc[K.up].wait()
+        hidden_rows(oc, hidO)
+        sends(K.h, [(K.h, hidO, hid2.at[pl.ds(TOK, TOK)], dc)])
+
+    @step
+    def hid2_():
+        hidden_rows(c, hid2)
+        for b in range(4):
+            ogT[b, :, 0:TOK] = og_ref[:, b * 256 : (b + 1) * 256].T
+
+    @step
     def A1():
         recv(K.Ax, Wb(y, ox, z, allr, cols(A)), dx)
         ref = Wb(y, allr, z, allr, cols(A))
@@ -218,10 +230,10 @@
         for o in (1, 3, 2):
             recv(f"Ay{o}", Wb(yy(-o), allr, z, allr, cols(A)), dy(-o))
         sends(K.A2, [
+            same(K.Az1L0, az(0, z), dz(-1)),
             same(K.Az1R0, az(0, z), dz(1)),
             same(K.Az1L1, az(1, z), dz(-1)),
             same(K.Az1R1, az(1, z), dz(1)),
-            same(K.Az1L0, az(0, z), dz(-1)),
             same(K.DA0, Wb(allr, allr, z, allr, cols(A)), dc),
         ])
 
@@ -236,11 +248,12 @@
 
         S[K.A3_ + nm] = f
 
-    last_a = (("3R1", 1, -3), ("3L0", 0, 3), ("4R0", 0, 4), ("4L1", 1, 4))
+    last_a = (("3R0", 0, -3), ("3R1", 1, -3), ("4L0", 0, 4), ("4L1", 1, 4))
     for s in (1, 2, 3):
-        for sd, h in ((K.R, 0), (K.L, 1), (K.R, 1), (K.L, 0)):
-            if s < 3 or (sd == K.R) == (h == 0):
-                a3(s, sd, h)
+        for h in (0, 1):
+            a3(s, K.L, h)
+            if s < 3:
+                a3(s, K.R, h)
 
     @step
     def A6():
@@ -345,15 +358,14 @@
 
     @step
     def RA1():
-        sa1[0] = ga(0, zz(4)).astype(BF)
-        sa1[1] = ga(1, zz(4)).astype(BF)
-        sa2[0, 0, 1] = ga(1, zz(3)).astype(BF)
-        sa2[1, 0, 0] = ga(0, zz(-3)).astype(BF)
+        for h in (0, 1):
+            sa1[h] = ga(h, zz(4)).astype(BF)
+            sa2[0, 0, h] = ga(h, zz(3)).astype(BF)
         sends(K.RA1, [
-            (K.rA1R0, sa1.at[0], ra1.at[0], dz(1)),
+            (K.rA1L0, sa1.at[0], ra1.at[0], dz(-1)),
             (K.rA1L1, sa1.at[1], ra1.at[1], dz(-1)),
+            (K.rA2R0, sa2.at[0, 0, 0], ra2.at[0, 0, 0], dz(1)),
             (K.rA2R1, sa2.at[0, 0, 1], ra2.at[0, 0, 1], dz(1)),
-            (K.rA2L0, sa2.at[1, 0, 0], ra2.at[1, 0, 0], dz(-1)),
         ])
 
     def ra(s, sd, h):
@@ -361,7 +373,7 @@
         side = 0 if sd == K.R else 1
 
         def f():
-            buf = ra1.at[side] if s == 2 else ra2.at[side, s - 3, h]
+            buf = ra1.at[h] if s == 2 else ra2.at[side, s - 3, h]
             recv(f"rA{s - 1}{sd}{h}", buf, dz(-sg))
             sa2[side, s - 2, h] = (ga(h, zz(sg * (5 - s))) + buf[...].astype(F32)).astype(BF)
             sends(K.RA, [(f"rA{s}{sd}{h}", sa2.at[side, s - 2, h], ra2.at[side, s - 2, h], dz(sg))])
@@ -370,7 +382,7 @@
 
     for sd in K.RL:
         for h in (0, 1):
-            for s in range(2 if (sd == K.R) == (h == 0) else 3, 5):
+            for s in range(2 if sd == K.L else 3, 5):
                 ra(s, sd, h)
 
     @step
@@ -527,7 +539,7 @@
             for s in (1, 2, 3, 4):
                 for sd, sg in ((K.R, 1), (K.L, -1)):
                     for h in (0, 1):
-                        if s < 4 or (sd == K.R) == (h == 0):
+                        if s < 4 or sd == K.L:
                             yield f"DA{s}{sd}{h}", W.at[oc, pl.ds(2 * h, 2), :, zz(-sg * s), :, cols(A)]
         if k == K.B:
             for nm, o, xi in (
@@ -579,8 +591,6 @@
             return 0
 
         lax.fori_loop(0, TOK // 16, body, 0)
-        local(f"gg{side}{k}", gg_ref.at[:, cs], gg_hbm.at[:, cs])
-        local(f"ug{side}{k}", ug_ref.at[:, cs], ug_hbm.at[:, cs])
 
     for side in K.co:
         for k in K.ABC:
@@ -598,7 +608,6 @@
         out_ref[...] = (
             acc[:, pl.ds(pl.multiple_of(r * 512, 128), 512)] + lo_r[...].astype(F32)
         ).astype(BF)
-        local(K.out, out_ref, out_hbm)
 
     def update(half, g):
         cs = pl.ds(pl.multiple_of(half * HALF, 128), HALF)
@@ -613,6 +622,8 @@
 
     @step
     def fin_():
+        loc[K.one].wait()
+        loc[K.two].wait()
         sends(K.fin, [(K.fin, fin.at[pl.ds(pl.multiple_of(oc * 8, 8), 8)], finP, dc)])
         update(c, fin[pl.ds(pl.multiple_of(c * 8, 8), 8), :])
 
@@ -620,21 +631,8 @@
     def adam():
         recv(K.fin, finP, dc)
         update(oc, finP[...])
-        local(K.mo, master_out, master_out_hbm)
-        local(K.oo, one_out, one_out_hbm)
-        local(K.to, two_out, two_out_hbm)
-
-    with jax.named_scope(K.loads):
-        loc[K.gate].wait()
-        loc[K.up].wait()
-    with jax.named_scope(K.hidden):
-        hidden_rows(oc, hidO)
-        hidden_rows(c, hid2)
-    for n in (K.og, K.master, K.one, K.two):
-        loc[n].wait()
-    with jax.named_scope(K.transpose):
-        for b in range(4):
-            ogT[b, :, 0:TOK] = og_ref[:, b * 256 : (b + 1) * 256].T
+
+    loc[K.master].wait()
     with jax.named_scope(K.barrier):
         pl.semaphore_wait(bar, len(peers))
     for n in ORDER:
@@ -644,9 +642,6 @@
     with jax.named_scope(K.sends_done):
         for d in sent:
             d.wait_send()
-        for n, d in loc.items():
-            if n not in (K.gate, K.up, K.og, K.master, K.one, K.two):
-                d.wait()
     assert len(slots) <= NSEM, len(slots)
 
 
@@ -654,46 +649,35 @@
 
 
 def copy_kernel(*refs):
-    src, dst, buf, sem = refs[0:6], refs[6:12], refs[12:18], refs[18]
-    parts = []
-    for i in (1, 2, 0, 3, 4, 5):
-        rows = src[i].shape[0]
-        n = 2 if rows > 8 else 1
-        for j in range(n):
-            rs = pl.ds(j * (rows // n), rows // n)
-            k = len(parts)
-            parts.append((
-                pltpu.make_async_copy(src[i].at[rs], buf[i].at[rs], sem.at[0, k]),
-                pltpu.make_async_copy(buf[i].at[rs], dst[i].at[rs], sem.at[1, k]),
-            ))
-    for a, _ in parts:
-        a.start()
-    for a, b in parts:
-        a.wait()
-        b.start()
-    for _, b in parts:
-        b.wait()
+    src, dst, sem = refs[0:6], refs[6:12], refs[12]
+    copies = [pltpu.make_async_copy(src[i], dst[i], sem.at[i]) for i in range(6)]
+    for d in copies:
+        d.start()
+    for d in copies:
+        d.wait()
 
 
 def on_device(gate_pre, up_pre, out_grad, master, moment_one, moment_two):
     V = pltpu.VMEM
+
+    def in_hbm(a):
+        return pltpu.with_memory_space_constraint(a, pltpu.HBM)
+
     nA, nB, nC = A[1], B[1], C[1]
     outs = pl.pallas_call(
         kernel,
         out_shape=(
-            jax.ShapeDtypeStruct((TOK, 512), BF),
-            jax.ShapeDtypeStruct((TOK, FF), BF),
-            jax.ShapeDtypeStruct((TOK, FF), BF),
-            jax.ShapeDtypeStruct((8, FF), F32),
-            jax.ShapeDtypeStruct((8, FF), F32),
-            jax.ShapeDtypeStruct((8, FF), F32),
+            V((TOK, 512), BF),
+            V((TOK, FF), BF),
+            V((TOK, FF), BF),
+            V((8, FF), F32),
+            V((8, FF), F32),
+            V((8, FF), F32),
         ),
-        in_specs=[pl.BlockSpec(memory_space=pl.ANY)] * 6,
-        out_specs=[pl.BlockSpec(memory_space=pl.ANY)] * 6,
+        in_specs=[pl.BlockSpec(memory_space=pltpu.HBM)] * 6,
+        out_specs=[pl.BlockSpec(memory_space=V)] * 6,
         scratch_shapes=[
             V((TOK, FF), BF), V((TOK, FF), BF), V((TOK, D), BF),
-            V((8, FF), F32), V((8, FF), F32), V((8, FF), F32),
-            V((TOK, 512), BF), V((TOK, FF), BF), V((TOK, FF), BF),
             V((8, FF), F32), V((8, FF), F32), V((8, FF), F32),
             V((NC, NY, NX, NZ, 16, HALF), BF),
             V((NY, NX, NZ, 16, HALF), F32),
@@ -725,23 +709,23 @@
             pltpu.SemaphoreType.DMA((24,)),
         ],
         compiler_params=pltpu.CompilerParams(
-            collective_id=0, has_side_effects=True, vmem_limit_bytes=66_000_000
+            collective_id=0, has_side_effects=True, vmem_limit_bytes=48_000_000
         ),
     )(
-        gate_pre.reshape(TOK, FF),
-        up_pre.reshape(TOK, FF),
-        out_grad.reshape(TOK, D),
-        master,
-        moment_one,
-        moment_two,
+        in_hbm(gate_pre.reshape(TOK, FF)),
+        in_hbm(up_pre.reshape(TOK, FF)),
+        in_hbm(out_grad.reshape(TOK, D)),
+        in_hbm(master),
+        in_hbm(moment_one),
+        in_hbm(moment_two),
     )
     outs = pl.pallas_call(
         copy_kernel,
         out_shape=tuple(jax.ShapeDtypeStruct(o.shape, o.dtype) for o in outs),
-        in_specs=[pl.BlockSpec(memory_space=pl.ANY)] * 6,
+        in_specs=[pl.BlockSpec(memory_space=V)] * 6,
         out_specs=[pl.BlockSpec(memory_space=pl.ANY)] * 6,
-        scratch_shapes=[V(o.shape, o.dtype) for o in outs] + [pltpu.SemaphoreType.DMA((2, 12))],
-    )(*outs)
+        scratch_shapes=[pltpu.SemaphoreType.DMA((6,))],
+    )(*[pltpu.with_memory_space_constraint(o, V) for o in outs])
     lo, gg, ug, mn, m1, m2 = outs
     return (
         lo.reshape(2, 128, 512),

time: 60.6 us -> 58.8 us (0.970)
  Pallas kernels: 59.4 us -> 58.1 us
    pallas_call x1, Pallas kernels: 3.06 us -> 1.79 us  [on_device(): pl.pallas_call(copy_kernel, out_shape=tuple((jax.ShapeDtypeStruct(o.shape...]
where the time goes in v3:
time: 58.8 us; the launch traced here: 58.7 us
  Pallas kernels  58.1 us (99%)
  between operations  0.64 us (1%)
    pallas_call x1, Pallas kernels, on_device(): pl.pallas_call(kernel, out_shape=(V((TOK, 512), BF), V((TOK, FF), BF), V(...  56.3 us
    pallas_call x1, Pallas kernels, on_device(): pl.pallas_call(copy_kernel, out_shape=tuple((jax.ShapeDtypeStruct(o.shape...  1.79 us

profile of v3, /device:TPU:1, one launch (start us, length us, event | category | flops | bytes accessed | tf_op | source)
XLA Modules:
  0.0 58.7 jit_solution(8341753930471546211)
XLA Ops:
  0.6 56.3 %shard_map.109 = (bf16[256,512]{1,0:T(8,128)(2,1)S(1)}, bf16[256,2816]{1,0:T(8,128)(2,1)S(1)}, bf16[256,2816]{1,0:T(8,128)(2,1)S(1)}, f32[8,2816]{1,0:T(8,128)S(...) custom-call(bf16[256,2816]{1,0:T(8,128)(2,1)} %bitcast.6, bf16[256,2816]{1,0:T(8,128)(2,1)} %bitcast.7, ...), custom_call_target="tpu_custom_call" | custom-call | tf_op jit(solution)/shard_map/pallas_call | solution.py:667
  56.9 1.8 %shard_map.110 = (bf16[256,512]{1,0:T(8,128)(2,1)}, bf16[256,2816]{1,0:T(8,128)(2,1)}, bf16[256,2816]{1,0:T(8,128)(2,1)}, f32[8,2816]{1,0:T(8,128)}, f32[8,2816]{1,0:T(8,128)}, /*index=5*/f32[8,2816]{1,0:T(8,128)}) custom-call(bf16[256,512]{1,0:T(8,128)(2,1)S(1)} %get-tuple-element.18.refs_0_, bf16[256,2816]{1,0:T(8,128)(2,1)S(1)} %get-tuple-element.19.refs_1_, ...), custom_call_target="tpu_custom_call" | custom-call | tf_op jit(solution)/shard_map/pallas_call | solution.py:722

commit v4 on v3

--- a/solution.py
+++ b/solution.py
@@ -1,3 +1,5 @@
+import math
+
 import jax
 import jax.numpy as jnp
 from jax import lax
@@ -36,42 +38,43 @@
 K = Names()
 
 ORDER = (
-    K.init, K.hidO_, K.A1, K.hid2_, K.gp, K.gB, K.RB1, K.gC, K.RC1, K.A2, K.gA, K.RA1, K.A3_1L1,
-    K.RB2L, K.A3_1L0, K.A3_1R1, K.BC1, K.RA3R1, K.RA2L0, K.A3_1R0, K.A3_2R1, K.A3_2L1, K.C2R,
-    K.A3_2L0, K.C2L, K.RB2R, K.RA4R1, K.A3_2R0, K.B2, K.A3_3L1, K.C3, K.RC2, K.A3_3L0, K.RA3R0,
-    K.RA2L1, K.RA3L0, K.B3R, K.B3L, K.RC2b, K.RC2c, K.A6, K.RB3, K.RA4R0, K.RA3L1, K.RA4L0,
-    K.C4, K.lo_cC, K.lo_oA, K.B4, K.RA4L1, K.lo_cB, K.lo_oC, K.lo_cA, K.RB4, K.lo_oB, K.losend,
-    K.RC3L, K.RC3R, K.hg_cB, K.RA5, K.hg_oA, K.RC4, K.hg_cA, K.hg_oC, K.hg_oB, K.RA6, K.hg_cC,
-    K.RB5, K.RC5, K.RA7, K.fin_, K.lofin, K.adam,
+    K.init, K.hidO_, K.hid2_, K.gp, K.gC, K.RC1, K.A1, K.gB, K.RB1, K.gA, K.RA1, K.BC1, K.A2,
+    K.RA3R1, K.RA2L1, K.A3_1R1, K.A3_1L0, K.A3_1R0, K.RA3R0, K.A3_1L1, K.RA2L0, K.C2L, K.A3_2L0,
+    K.C2R, K.B2, K.A3_2L1, K.RB2L, K.B3R, K.RA4R0, K.A3_3L0, K.RB2R, K.RA3L0, K.A3_3L1, K.B3L,
+    K.A3_2R1, K.A3_2R0, K.RA3L1, K.RC2, K.C3, K.RB3, K.RA4R1, K.RA4L0, K.C4, K.lo_cC, K.A6,
+    K.B4, K.lo_cB, K.RC2b, K.RA4L1, K.lo_cA, K.lo_oC, K.RC2c, K.lo_oA, K.RB4, K.lo_oB, K.losend,
+    K.RC3R, K.RC3L, K.RA5, K.RC4, K.hg_oB0, K.hg_oB1, K.hg_oA1, K.hg_oC1, K.hg_cC0, K.hg_cA1,
+    K.RA6, K.hg_oC0, K.hg_cB0, K.hg_oA0, K.hg_cC1, K.hg_cB1, K.hg_cA0, K.RB5, K.RC5, K.RA7,
+    K.fin_, K.lofin, K.adam,
 )
 ORDS = {
-    K.init: (K.Zd2, K.Zd6, K.Zd3, K.Zd4, K.og, K.Zd1, K.Zd7, K.Zd5, K.Ax,),
-    K.A1: (K.Ay2, K.Ay1, K.Ay3,),
-    K.A2: (K.Az1L1, K.DA0, K.Az1L0, K.Az1R1, K.Az1R0,),
-    K.A3_1R0: (K.DA1R0, K.Az2R0,),
-    K.A3_1R1: (K.Az2R1, K.DA1R1,),
+    K.init: (K.Zd3, K.Zd5, K.Zd7, K.og, K.Zd4, K.Ax, K.Zd6, K.Zd2, K.Zd1,),
+    K.A1: (K.Ay3, K.Ay1, K.Ay2,),
+    K.A2: (K.Az1R1, K.DA0, K.Az1L0, K.Az1R0, K.Az1L1,),
+    K.A3_1R0: (K.Az2R0, K.DA1R0,),
+    K.A3_1R1: (K.DA1R1, K.Az2R1,),
     K.A3_1L0: (K.Az2L0, K.DA1L0,),
-    K.A3_1L1: (K.DA1L1, K.Az2L1,),
+    K.A3_1L1: (K.Az2L1, K.DA1L1,),
     K.A3_2R0: (K.DA2R0, K.Az3R0,),
-    K.A3_2R1: (K.Az3R1, K.DA2R1,),
-    K.A3_2L0: (K.Az3L0, K.DA2L0,),
+    K.A3_2R1: (K.DA2R1, K.Az3R1,),
+    K.A3_2L0: (K.DA2L0, K.Az3L0,),
     K.A3_2L1: (K.Az3L1, K.DA2L1,),
-    K.A3_3L0: (K.Az4L0, K.DA3L0,),
-    K.A3_3L1: (K.DA3L1, K.Az4L1,),
-    K.BC1: (K.Cy1L, K.Cy1R, K.Bx, K.DB0, K.Cx0, K.By1Rx, K.DC0, K.By1Lx,),
+    K.A3_3L0: (K.DA3L0, K.Az4L0,),
+    K.A3_3L1: (K.Az4L1, K.DA3L1,),
+    K.BC1: (K.DC0, K.Bx, K.Cx0, K.Cy1L, K.Cy1R, K.DB0, K.By1Rx, K.By1Lx,),
     K.B2: (K.By1Ro, K.DB1, K.By1Lo,),
-    K.B3R: (K.DB2, K.By2R,),
-    K.B3L: (K.DB3, K.By2L,),
-    K.C2R: (K.DC3, K.Cy2R, K.Cx3,),
-    K.C2L: (K.Cx1, K.Cy2L, K.DC1,),
+    K.B3R: (K.By2R, K.DB2,),
+    K.B3L: (K.By2L, K.DB3,),
+    K.C2R: (K.Cx3, K.Cy2R, K.DC3,),
+    K.C2L: (K.DC1, K.Cx1, K.Cy2L,),
     K.C3: (K.Cx2, K.DC2,),
-    K.RC1: (K.rCx3, K.rCx2, K.rCx0, K.rCx1,),
-    K.RB1: (K.rB1R, K.rB1L, K.rB2L1, K.rB2R1,),
-    K.RA1: (K.rA2R1, K.rA1L1, K.rA2R0, K.rA1L0,),
-    K.RA5: (K.rAy3, K.rAy1, K.rAy2,),
-    K.RB4: (K.rBz7, K.rBz1, K.rBz4, K.rBz2, K.rBz6, K.rBz5, K.rBz3,),
+    K.RC1: (K.rCx3, K.rCx2, K.rCx1, K.rCx0,),
+    K.RB1: (K.rB1R, K.rB2R1, K.rB2L1, K.rB1L,),
+    K.RA1: (K.rA2R1, K.rA2R0, K.rA1L0, K.rA1L1,),
+    K.RA5: (K.rAy1, K.rAy2, K.rAy3,),
+    K.RB4: (K.rBz3, K.rBz5, K.rBz7, K.rBz6, K.rBz2, K.rBz1, K.rBz4,),
     K.RC2: (K.rCy1R, K.rCy1L,),
-    K.RC4: (K.rCz4, K.rCz5, K.rCz3, K.rCz2, K.rCz6, K.rCz1, K.rCz7,),
+    K.RC4: (K.rCz4, K.rCz3, K.rCz1, K.rCz7, K.rCz6, K.rCz2, K.rCz5,),
 }
 
 
@@ -83,7 +86,7 @@
     sa1, ra1, sa2, ra2, sa3, ra3, sa4, ra4,
     sb1, rb1, sb2, rb2, sb3, rb3, sb4, rb4,
     sc1, rc1, sc2, rc2, sc3, rc3, sc4, rc4,
-    ssem, rsem, lsem,
+    space, ssem, rsem, lsem,
 ):
     y = lax.axis_index(K.dp_0)
     x = lax.axis_index(K.dp_1)
@@ -129,20 +132,27 @@
     local(K.one, one_hbm, one_ref)
     local(K.two, two_hbm, two_ref)
 
-    sent = []
-    slots = {}
-
-    def slot(name):
-        if name not in slots:
-            slots[name] = len(slots)
-        return slots[name]
+    slots, sent, arriving = {}, {}, {}
+
+    def size(ref):
+        return math.prod(ref.shape) * ref.dtype.itemsize
 
     def rc(name, src, dst, dev):
-        k = slot(name)
+        group = group_of(name)
+        k = slots.setdefault(group, len(slots))
+        sent.setdefault(size(src), 0)
         return pltpu.make_async_remote_copy(
-            src_ref=src, dst_ref=dst, send_sem=ssem.at[k], recv_sem=rsem.at[k],
-            device_id=dev, device_id_type=pl.DeviceIdType.MESH,
+            src_ref=src, dst_ref=dst, send_sem=ssem.at[list(sent).index(size(src))],
+            recv_sem=rsem.at[k], device_id=dev, device_id_type=pl.DeviceIdType.MESH,
         )
+
+    def tiles(total):
+        return space.at[pl.ds(0, total // 4096)]
+
+    def recv_all(group):
+        n = arriving[group]
+        with jax.named_scope(K.wait_ + group):
+            rc(group, tiles(n), tiles(n), dc).wait_recv()
 
     def sends(step, items):
         names = ORDS.get(step, tuple(i[0] for i in items))
@@ -151,9 +161,9 @@
             table[n]
         for name in list(names) + [n for n in table if n not in names]:
             _, src, dst, dev = table[name]
-            d = rc(name, src, dst, dev)
-            d.start()
-            sent.append(d)
+            rc(name, src, dst, dev).start()
+            sent[size(src)] += 1
+            arriving[group_of(name)] = arriving.get(group_of(name), 0) + size(dst)
 
     def recv(name, dst, dev):
         with jax.named_scope(K.wait_ + name):
@@ -227,8 +237,7 @@
 
     @step
     def A2():
-        for o in (1, 3, 2):
-            recv(f"Ay{o}", Wb(yy(-o), allr, z, allr, cols(A)), dy(-o))
+        recv_all(K.Ay)
         sends(K.A2, [
             same(K.Az1L0, az(0, z), dz(-1)),
             same(K.Az1R0, az(0, z), dz(1)),
@@ -257,8 +266,7 @@
 
     @step
     def A6():
-        for nm, h, o in last_a:
-            recv(K.Az + nm, az(h, zz(o)), dz(-1 if K.R in nm else 1))
+        recv_all(K.Az9)
         sends(K.A6, [same(K.DA + nm, az(h, zz(o)), dc) for nm, h, o in last_a])
 
     def bref(yi, xi):
@@ -269,8 +277,7 @@
 
     @step
     def BC1():
-        for o in (1, 7, 2, 6, 3, 5, 4):
-            recv(f"Zd{o}", Wb(y, x, zz(-o), allr, cols(BC)), dz(-o))
+        recv_all(K.Zd)
         b, cc = bref(y, x), cref(y, x)
         sends(K.BC1, [
             same(K.Bx, b, dx), same(K.By1Rx, b, dy(1)), same(K.By1Lx, b, dy(-1)),
@@ -300,8 +307,7 @@
 
     @step
     def B4():
-        for nm, o, xi, d in last_b:
-            recv(nm, bref(yy(o), xi), dy(d))
+        recv_all(K.By9)
         sends(K.B4, [same(K.D + nm, bref(yy(o), xi), dc) for nm, o, xi, d in last_b])
 
     lo4, hi4 = pl.ds(0, 4), pl.ds(4, 4)
@@ -324,14 +330,12 @@
 
     @step
     def C3():
-        recv(K.Cy2R, cref(yy(2), x, lo4), dy(-1))
-        recv(K.Cy2L, cref(yy(2), x, hi4), dy(1))
+        recv_all(K.Cy2)
         sends(K.C3, [same(K.Cx2, cref(yy(2), x), dx), same(K.DC2, cref(yy(2), x), dc)])
 
     @step
     def C4():
-        for o in (0, 1, 3, 2):
-            recv(f"Cx{o}", cref(yy(o), ox), dx)
+        recv_all(K.Cx)
         sends(K.C4, [same(f"DCx{o}", cref(yy(o), ox), dc) for o in (0, 1, 3, 2)])
 
     @step
@@ -342,12 +346,12 @@
         recv(K.h, hid2.at[pl.ds(TOK, TOK)], dc)
 
     def grads(cr):
-        def body(b, _):
-            p = jnp.dot(ogT[b], hid2[:, cols(cr)], preferred_element_type=F32)
-            G[b, :, :, :, cols(cr)] = p.reshape(NX, NZ, 16, cr[1])
-            return 0
-
-        lax.fori_loop(0, NY, body, 0)
+        for c0 in range(cr[0], cr[0] + cr[1], 256):
+            n = min(256, cr[0] + cr[1] - c0)
+            p = jnp.dot(
+                ogT[...].reshape(D, 2 * TOK), hid2[:, pl.ds(c0, n)], preferred_element_type=F32
+            )
+            G[:, :, :, :, pl.ds(c0, n)] = p.reshape(NY, NX, NZ, 16, n)
 
     S[K.gA] = lambda: grads(A)
     S[K.gB] = lambda: grads(B)
@@ -387,9 +391,7 @@
 
     @step
     def RA5():
-        for sd, d in ((K.R, -1), (K.L, 1)):
-            for h in (0, 1):
-                recv(f"rA4{sd}{h}", ra2.at[K.RL.index(sd), 2, h], dz(d))
+        recv_all(K.rA4)
         for h in (0, 1):
             t = ga(h, z) + ra2[0, 2, h].astype(F32) + ra2[1, 2, h].astype(F32)
             G[2 * h : 2 * h + 2, :, z, :, cols(A)] = t
@@ -398,8 +400,7 @@
 
     @step
     def RA6():
-        for o in (1, 3, 2):
-            recv(f"rAy{o}", ra3.at[o - 1], dy(-o))
+        recv_all(K.rAy)
         t = G[y, :, z, :, cols(A)]
         for o in (1, 2, 3):
             t = t + ra3[o - 1].astype(F32)
@@ -441,16 +442,13 @@
 
     @step
     def RB3():
-        recv(K.rB2R1, rb2.at[0, 1], dy(-1))
-        recv(K.rB2L0, rb2.at[1, 1], dy(1))
+        recv_all(K.rB3)
         sb3[...] = (gb(y, ox) + rb2[0, 1].astype(F32) + rb2[1, 1].astype(F32)).astype(BF)
         sends(K.RB3, [(K.rBx, sb3, rb3, dx)])
 
     @step
     def RB4():
-        recv(K.rB2R0, rb2.at[0, 0], dy(-1))
-        recv(K.rB2L1, rb2.at[1, 0], dy(1))
-        recv(K.rBx, rb3, dx)
+        recv_all(K.rB4)
         t = gb(y, x) + rb2[0, 0].astype(F32) + rb2[1, 0].astype(F32) + rb3[...].astype(F32)
         G[y, x, :, :, cols(B)] = t
         sb4[...] = t.astype(BF)
@@ -459,8 +457,7 @@
     @step
     def RB5():
         t = G[y, x, z, :, cols(B)]
-        for o in range(1, NZ):
-            recv(f"rBz{o}", rb4.at[o - 1], dz(-o))
+        recv_all(K.rBz)
         for o in range(1, NZ):
             t = t + rb4[o - 1].astype(F32)
         fin[:, cols(B)] = t
@@ -514,11 +511,7 @@
 
     @step
     def RC4():
-        recv(K.rCx0, rc1.at[0], dx)
-        recv(K.rCy2R0, rc3.at[0, lo4], dy(-1))
-        recv(K.rCy2R1, rc3.at[0, hi4], dy(-1))
-        recv(K.rCy2L0, rc3.at[1, hi4], dy(1))
-        recv(K.rCy2L1, rc3.at[1, lo4], dy(1))
+        recv_all(K.rC4)
         t = gc(y, x) + rc1[0].astype(F32) + rc3[0].astype(F32) + rc3[1].astype(F32)
         G[y, x, :, :, cols(C)] = t
         sc4[...] = t.astype(BF)
@@ -527,45 +520,24 @@
     @step
     def RC5():
         t = G[y, x, z, :, cols(C)]
-        for o in range(1, NZ):
-            recv(f"rCz{o}", rc4.at[o - 1], dz(-o))
+        recv_all(K.rCz)
         for o in range(1, NZ):
             t = t + rc4[o - 1].astype(F32)
         fin[:, cols(C)] = t
 
-    def partner_pieces(k):
-        if k == K.A:
-            yield K.DA0, W.at[oc, :, :, z, :, cols(A)]
-            for s in (1, 2, 3, 4):
-                for sd, sg in ((K.R, 1), (K.L, -1)):
-                    for h in (0, 1):
-                        if s < 4 or sd == K.L:
-                            yield f"DA{s}{sd}{h}", W.at[oc, pl.ds(2 * h, 2), :, zz(-sg * s), :, cols(A)]
-        if k == K.B:
-            for nm, o, xi in (
-                (K.DB0, 0, x), (K.DB1, 0, ox), (K.DB2, -1, x), (K.DB3, 1, ox),
-                (K.DBy1Ro, -1, ox), (K.DBy1Lx, 1, x), (K.DBy2R, 2, x), (K.DBy2L, 2, ox),
-            ):
-                yield nm, W.at[oc, yy(o), xi, :, :, cols(B)]
-        if k == K.C:
-            for o in (0, 1, 3, 2):
-                yield f"DC{o}", W.at[oc, yy(o), x, :, :, cols(C)]
-                yield f"DCx{o}", W.at[oc, yy(o), ox, :, :, cols(C)]
-
     ranges = {K.A: A, K.B: B, K.C: C}
     have = set()
     started = []
 
-    def w_of(side, k):
+    def w_of(side, k, c0, n):
         if side == K.o and k not in have:
             have.add(k)
-            for nm, ref in partner_pieces(k):
-                recv(nm, ref, dc)
+            recv_all(K.D + k)
         half = c if side == K.c else oc
-        return W[half, :, :, :, :, cols(ranges[k])].reshape(D, ranges[k][1])
+        return W[half, :, :, :, :, pl.ds(c0, n)].reshape(D, n)
 
     def lo(side, k):
-        w = w_of(side, k)
+        w = w_of(side, k, *ranges[k])
         h = (hid2 if side == K.c else hidO)[0:TOK, cols(ranges[k])]
         part = lax.dot_general(h, w, (((1,), (1,)), ((), ())), preferred_element_type=F32)
         if started:
@@ -574,11 +546,12 @@
             acc[...] = part
         started.append(1)
 
-    def hgrad(side, k):
-        n = ranges[k][1]
+    def hgrad(side, k, j):
+        c0 = ranges[k][0] + 256 * j
+        n = min(256, ranges[k][1] - 256 * j)
         half = c if side == K.c else oc
-        hg[:, 0:n] = jnp.dot(og_ref[...], w_of(side, k), preferred_element_type=F32)
-        cs = pl.ds(pl.multiple_of(half * HALF + ranges[k][0], 128), n)
+        hg[:, 0:n] = jnp.dot(og_ref[...], w_of(side, k, c0, n), preferred_element_type=F32)
+        cs = pl.ds(pl.multiple_of(half * HALF + c0, 128), n)
 
         def body(i, _):
             rows = pl.ds(pl.multiple_of(i * 16, 16), 16)
@@ -595,7 +568,8 @@
     for side in K.co:
         for k in K.ABC:
             S[f"lo_{side}{k}"] = lambda side=side, k=k: lo(side, k)
-            S[f"hg_{side}{k}"] = lambda side=side, k=k: hgrad(side, k)
+            for j in range(-(-ranges[k][1] // 256)):
+                S[f"hg_{side}{k}{j}"] = lambda side=side, k=k, j=j: hgrad(side, k, j)
 
     @step
     def losend():
@@ -640,12 +614,38 @@
             S.pop(n)()
     assert not S, S.keys()
     with jax.named_scope(K.sends_done):
-        for d in sent:
-            d.wait_send()
-    assert len(slots) <= NSEM, len(slots)
-
-
-NSEM = 144
+        for n, many in sent.items():
+            if many:
+                pltpu.make_async_remote_copy(
+                    src_ref=tiles(n * many), dst_ref=tiles(n * many),
+                    send_sem=ssem.at[list(sent).index(n)], recv_sem=rsem.at[0],
+                    device_id=dc, device_id_type=pl.DeviceIdType.MESH,
+                ).wait_send()
+    assert len(slots) <= NRECV and len(sent) <= NSEND, (len(slots), len(sent))
+
+
+NRECV, NSEND = 56, 20
+
+GROUPS = {}
+for _first, _names in (
+    (K.Az9, (K.Az3R0, K.Az3R1, K.Az4L0, K.Az4L1)),
+    (K.By9, (K.By2R, K.By2L, K.By1Ro, K.By1Lx)),
+    (K.rB4, (K.rB2R0, K.rB2L1, K.rBx)),
+    (K.rB3, (K.rB2R1, K.rB2L0)),
+    (K.rC4, (K.rCx0, K.rCy2R0, K.rCy2R1, K.rCy2L0, K.rCy2L1)),
+    (K.Cy2, (K.Cy2R, K.Cy2L)),
+):
+    for _n in _names:
+        GROUPS[_n] = _first
+
+
+def group_of(name):
+    if name in GROUPS:
+        return GROUPS[name]
+    for p in (K.Zd, K.Ay, K.rAy, K.rBz, K.rCz, K.DA, K.DB, K.DC, K.Cx, K.rA4):
+        if name.startswith(p):
+            return p
+    return name
 
 
 def copy_kernel(*refs):
@@ -704,9 +704,10 @@
             V((NZ, 16, nC), BF), V((2, 4, 16, nC), BF),
             V((2, NZ, 16, nC), BF), V((2, NZ, 16, nC), BF),
             V((NZ, 16, nC), BF), V((7, 16, nC), BF),
-            pltpu.SemaphoreType.DMA((NSEM,)),
-            pltpu.SemaphoreType.DMA((NSEM,)),
-            pltpu.SemaphoreType.DMA((24,)),
+            V((768, 16, 128), BF),
+            pltpu.SemaphoreType.DMA((NSEND,)),
+            pltpu.SemaphoreType.DMA((NRECV,)),
+            pltpu.SemaphoreType.DMA((6,)),
         ],
         compiler_params=pltpu.CompilerParams(
             collective_id=0, has_side_effects=True, vmem_limit_bytes=48_000_000

time: 58.8 us -> 58 us (0.986)
  Pallas kernels: 58.1 us -> 57.3 us
    pallas_call x1, Pallas kernels: 56.3 us -> 55.5 us  [on_device(): pl.pallas_call(kernel, out_shape=(V((TOK, 512), BF), V((TOK, FF), BF), V(...]
where the time goes in v4:
time: 58 us; the launch traced here: 57.9 us
  Pallas kernels  57.3 us (99%)
  between operations  0.64 us (1%)
    pallas_call x1, Pallas kernels, on_device(): pl.pallas_call(kernel, out_shape=(V((TOK, 512), BF), V((TOK, FF), BF), V(...  55.5 us
    pallas_call x1, Pallas kernels, on_device(): pl.pallas_call(copy_kernel, out_shape=tuple((jax.ShapeDtypeStruct(o.shape...  1.79 us

profile of v4, /device:TPU:1, one launch (start us, length us, event | category | flops | bytes accessed | tf_op | source)
XLA Modules:
  0.0 57.9 jit_solution(15062686042904986234)
XLA Ops:
  0.6 55.5 %shard_map.109 = (bf16[256,512]{1,0:T(8,128)(2,1)S(1)}, bf16[256,2816]{1,0:T(8,128)(2,1)S(1)}, bf16[256,2816]{1,0:T(8,128)(2,1)S(1)}, f32[8,2816]{1,0:T(8,128)S(...) custom-call(bf16[256,2816]{1,0:T(8,128)(2,1)} %bitcast.6, bf16[256,2816]{1,0:T(8,128)(2,1)} %bitcast.7, ...), custom_call_target="tpu_custom_call" | custom-call | tf_op jit(solution)/shard_map/pallas_call | solution.py:667
  56.2 1.8 %shard_map.110 = (bf16[256,512]{1,0:T(8,128)(2,1)}, bf16[256,2816]{1,0:T(8,128)(2,1)}, bf16[256,2816]{1,0:T(8,128)(2,1)}, f32[8,2816]{1,0:T(8,128)}, f32[8,2816]{1,0:T(8,128)}, /*index=5*/f32[8,2816]{1,0:T(8,128)}) custom-call(bf16[256,512]{1,0:T(8,128)(2,1)S(1)} %get-tuple-element.18.refs_0_, bf16[256,2816]{1,0:T(8,128)(2,1)S(1)} %get-tuple-element.19.refs_1_, ...), custom_call_target="tpu_custom_call" | custom-call | tf_op jit(solution)/shard_map/pallas_call | solution.py:723

commit v5 on v4

--- a/solution.py
+++ b/solution.py
@@ -38,51 +38,52 @@
 K = Names()
 
 ORDER = (
-    K.init, K.hidO_, K.hid2_, K.gp, K.gC, K.RC1, K.A1, K.gB, K.RB1, K.gA, K.RA1, K.BC1, K.A2,
-    K.RA3R1, K.RA2L1, K.A3_1R1, K.A3_1L0, K.A3_1R0, K.RA3R0, K.A3_1L1, K.RA2L0, K.C2L, K.A3_2L0,
-    K.C2R, K.B2, K.A3_2L1, K.RB2L, K.B3R, K.RA4R0, K.A3_3L0, K.RB2R, K.RA3L0, K.A3_3L1, K.B3L,
-    K.A3_2R1, K.A3_2R0, K.RA3L1, K.RC2, K.C3, K.RB3, K.RA4R1, K.RA4L0, K.C4, K.lo_cC, K.A6,
-    K.B4, K.lo_cB, K.RC2b, K.RA4L1, K.lo_cA, K.lo_oC, K.RC2c, K.lo_oA, K.RB4, K.lo_oB, K.losend,
-    K.RC3R, K.RC3L, K.RA5, K.RC4, K.hg_oB0, K.hg_oB1, K.hg_oA1, K.hg_oC1, K.hg_cC0, K.hg_cA1,
-    K.RA6, K.hg_oC0, K.hg_cB0, K.hg_oA0, K.hg_cC1, K.hg_cB1, K.hg_cA0, K.RB5, K.RC5, K.RA7,
-    K.fin_, K.lofin, K.adam,
+    K.init, K.hidO_, K.hid2_, K.gp, K.gC0, K.gC1, K.RC1, K.A1, K.gB0, K.gB1, K.RB1, K.gA0,
+    K.gA1, K.RA1, K.A2, K.RA2L0, K.BC1, K.RA3R1, K.A3_1L0, K.A3_1R1, K.RA2L1, K.RA3L0, K.A3_1R0,
+    K.C2R, K.C2L, K.fc, K.A3_1L1, K.B2, K.RA3R0, K.RB2L, K.A3_2L0, K.A3_2L1, K.A3_2R1, K.RA4R0,
+    K.A3_2R0, K.B3R, K.B3L, K.RC2, K.C3, K.A3_3L0, K.fo, K.A3_3L1, K.RA3L1, K.RB2R, K.RB3,
+    K.RC2b, K.RC2c, K.C4, K.hg_cC0, K.RA4R1, K.lo_cC, K.RC3R, K.RA4L0, K.A6, K.B4, K.lo_oC,
+    K.lo_cA, K.RA4L1, K.lo_cB, K.lo_oA, K.RB4, K.lo_oB, K.losend, K.RC3L, K.hg_oB0, K.hg_oA1,
+    K.RA5, K.RC4, K.hg_cA1, K.hg_oB1, K.hg_cB0, K.hg_oC0, K.hg_cC1, K.RA6, K.hg_cA0, K.hg_cB1,
+    K.RB5, K.hg_oA0, K.RA7, K.RC5, K.fin_, K.hg_oC1, K.lofin, K.adam,
 )
 ORDS = {
-    K.init: (K.Zd3, K.Zd5, K.Zd7, K.og, K.Zd4, K.Ax, K.Zd6, K.Zd2, K.Zd1,),
+    K.init: (K.Zd7, K.Zd5, K.Zd6, K.Zd1, K.Ax, K.og, K.Zd3, K.Zd4, K.Zd2,),
     K.A1: (K.Ay3, K.Ay1, K.Ay2,),
-    K.A2: (K.Az1R1, K.DA0, K.Az1L0, K.Az1R0, K.Az1L1,),
-    K.A3_1R0: (K.Az2R0, K.DA1R0,),
+    K.A2: (K.Az1L0, K.DA0, K.Az1R1, K.Az1L1, K.Az1R0,),
+    K.A3_1R0: (K.DA1R0, K.Az2R0,),
     K.A3_1R1: (K.DA1R1, K.Az2R1,),
-    K.A3_1L0: (K.Az2L0, K.DA1L0,),
+    K.A3_1L0: (K.DA1L0, K.Az2L0,),
     K.A3_1L1: (K.Az2L1, K.DA1L1,),
-    K.A3_2R0: (K.DA2R0, K.Az3R0,),
-    K.A3_2R1: (K.DA2R1, K.Az3R1,),
+    K.A3_2R0: (K.Az3R0, K.DA2R0,),
+    K.A3_2R1: (K.Az3R1, K.DA2R1,),
     K.A3_2L0: (K.DA2L0, K.Az3L0,),
-    K.A3_2L1: (K.Az3L1, K.DA2L1,),
-    K.A3_3L0: (K.DA3L0, K.Az4L0,),
+    K.A3_2L1: (K.DA2L1, K.Az3L1,),
+    K.A3_3L0: (K.Az4L0, K.DA3L0,),
     K.A3_3L1: (K.Az4L1, K.DA3L1,),
-    K.BC1: (K.DC0, K.Bx, K.Cx0, K.Cy1L, K.Cy1R, K.DB0, K.By1Rx, K.By1Lx,),
+    K.BC1: (K.Bx, K.Cy1L, K.DC0, K.Cx0, K.DB0, K.By1Lx, K.Cy1R, K.By1Rx,),
     K.B2: (K.By1Ro, K.DB1, K.By1Lo,),
     K.B3R: (K.By2R, K.DB2,),
     K.B3L: (K.By2L, K.DB3,),
-    K.C2R: (K.Cx3, K.Cy2R, K.DC3,),
-    K.C2L: (K.DC1, K.Cx1, K.Cy2L,),
+    K.C2R: (K.Cx3, K.DC3, K.Cy2R,),
+    K.C2L: (K.DC1, K.Cy2L, K.Cx1,),
     K.C3: (K.Cx2, K.DC2,),
-    K.RC1: (K.rCx3, K.rCx2, K.rCx1, K.rCx0,),
-    K.RB1: (K.rB1R, K.rB2R1, K.rB2L1, K.rB1L,),
-    K.RA1: (K.rA2R1, K.rA2R0, K.rA1L0, K.rA1L1,),
-    K.RA5: (K.rAy1, K.rAy2, K.rAy3,),
-    K.RB4: (K.rBz3, K.rBz5, K.rBz7, K.rBz6, K.rBz2, K.rBz1, K.rBz4,),
+    K.RC1: (K.rCx0, K.rCx2, K.rCx1, K.rCx3,),
+    K.RB1: (K.rB1L, K.rB2R1, K.rB2L1, K.rB1R,),
+    K.RA1: (K.rA1L0, K.rA2R1, K.rA1L1, K.rA2R0,),
+    K.RA5: (K.rAy2, K.rAy1, K.rAy3,),
+    K.RB4: (K.rBz1, K.rBz5, K.rBz6, K.rBz7, K.rBz2, K.rBz3, K.rBz4,),
     K.RC2: (K.rCy1R, K.rCy1L,),
-    K.RC4: (K.rCz4, K.rCz3, K.rCz1, K.rCz7, K.rCz6, K.rCz2, K.rCz5,),
+    K.RC4: (K.rCz7, K.rCz6, K.rCz4, K.rCz3, K.rCz1, K.rCz2, K.rCz5,),
 }
+HORDER = (K.C, K.B, K.A)
 
 
 def kernel(
     gate_hbm, up_hbm, og_hbm, master_hbm, one_hbm, two_hbm,
     out_ref, gg_ref, ug_ref, master_out, one_out, two_out,
     gate_ref, up_ref, og_ref, master_ref, one_ref, two_ref,
-    W, G, hid2, hidO, ogP, ogT, mP, hg, acc, fin, finP, lo_s, lo_r,
+    W, G, hid2, hidO, ogP, ogT, mP, fg, fu, acc, fin, finP, lo_s, lo_r,
     sa1, ra1, sa2, ra2, sa3, ra3, sa4, ra4,
     sb1, rb1, sb2, rb2, sb3, rb3, sb4, rb4,
     sc1, rc1, sc2, rc2, sc3, rc3, sc4, rc4,
@@ -169,15 +170,29 @@
         with jax.named_scope(K.wait_ + name):
             rc(name, dst, dst, dev).wait_recv()
 
-    def hidden_rows(half, out):
-        off = pl.multiple_of(half * HALF, 128)
+    def hidden_rows(half, out, cr):
+        cs = pl.ds(pl.multiple_of(half * HALF + cr[0], 128), cr[1])
+
+        def body(i, _):
+            rows = pl.ds(pl.multiple_of(i * 32, 32), 32)
+            g = gate_ref[rows, cs].astype(F32)
+            u = up_ref[rows, cs].astype(F32)
+            s = jax.nn.sigmoid(g)
+            out[rows, cols(cr)] = (g * s * u).astype(BF)
+            return 0
+
+        lax.fori_loop(0, TOK // 32, body, 0)
+
+    def factor_rows(half):
+        cs = pl.ds(pl.multiple_of(half * HALF, 128), HALF)
 
         def body(i, _):
             rows = pl.ds(pl.multiple_of(i * 16, 16), 16)
-            g = gate_ref[rows, pl.ds(off, HALF)].astype(F32)
-            u = up_ref[rows, pl.ds(off, HALF)].astype(F32)
+            g = gate_ref[rows, cs].astype(F32)
+            u = up_ref[rows, cs].astype(F32)
             s = jax.nn.sigmoid(g)
-            out[rows, :] = (g * s * u).astype(BF)
+            fg[half, rows, :] = u * s * (1.0 + g * (1.0 - s))
+            fu[half, rows, :] = g * s
             return 0
 
         lax.fori_loop(0, TOK // 16, body, 0)
@@ -188,6 +203,7 @@
     def same(name, ref, dev):
         return (name, ref, ref, dev)
 
+    ranges = {K.A: A, K.B: B, K.C: C}
     S = {}
 
     def step(f):
@@ -217,14 +233,20 @@
     def hidO_():
         loc[K.gate].wait()
         loc[K.up].wait()
-        hidden_rows(oc, hidO)
-        sends(K.h, [(K.h, hidO, hid2.at[pl.ds(TOK, TOK)], dc)])
+        for k in HORDER:
+            cr = ranges[k]
+            hidden_rows(oc, hidO, cr)
+            sends(K.h, [(K.h + k, hidO.at[:, cols(cr)], hid2.at[pl.ds(TOK, TOK), cols(cr)], dc)])
 
     @step
     def hid2_():
-        hidden_rows(c, hid2)
+        for k in HORDER:
+            hidden_rows(c, hid2, ranges[k])
         for b in range(4):
             ogT[b, :, 0:TOK] = og_ref[:, b * 256 : (b + 1) * 256].T
+
+    S[K.fo] = lambda: factor_rows(oc)
+    S[K.fc] = lambda: factor_rows(c)
 
     @step
     def A1():
@@ -343,19 +365,21 @@
         recv(K.og, ogP, dc)
         for b in range(4):
             ogT[b, :, TOK : 2 * TOK] = ogP[:, b * 256 : (b + 1) * 256].T
-        recv(K.h, hid2.at[pl.ds(TOK, TOK)], dc)
-
-    def grads(cr):
-        for c0 in range(cr[0], cr[0] + cr[1], 256):
-            n = min(256, cr[0] + cr[1] - c0)
-            p = jnp.dot(
-                ogT[...].reshape(D, 2 * TOK), hid2[:, pl.ds(c0, n)], preferred_element_type=F32
-            )
-            G[:, :, :, :, pl.ds(c0, n)] = p.reshape(NY, NX, NZ, 16, n)
-
-    S[K.gA] = lambda: grads(A)
-    S[K.gB] = lambda: grads(B)
-    S[K.gC] = lambda: grads(C)
+
+    def grads(k, j):
+        cr = ranges[k]
+        if j == 0:
+            recv(K.h + k, hid2.at[pl.ds(TOK, TOK), cols(cr)], dc)
+        c0 = cr[0] + 256 * j
+        n = min(256, cr[1] - 256 * j)
+        p = jnp.dot(
+            ogT[...].reshape(D, 2 * TOK), hid2[:, pl.ds(c0, n)], preferred_element_type=F32
+        )
+        G[:, :, :, :, pl.ds(c0, n)] = p.reshape(NY, NX, NZ, 16, n)
+
+    for k in K.ABC:
+        for j in range(-(-ranges[k][1] // 256)):
+            S[f"g{k}{j}"] = lambda k=k, j=j: grads(k, j)
 
     def ga(h, zi):
         return G[2 * h : 2 * h + 2, :, zi, :, cols(A)]
@@ -525,7 +549,6 @@
             t = t + rc4[o - 1].astype(F32)
         fin[:, cols(C)] = t
 
-    ranges = {K.A: A, K.B: B, K.C: C}
     have = set()
     started = []
 
@@ -550,20 +573,10 @@
         c0 = ranges[k][0] + 256 * j
         n = min(256, ranges[k][1] - 256 * j)
         half = c if side == K.c else oc
-        hg[:, 0:n] = jnp.dot(og_ref[...], w_of(side, k, c0, n), preferred_element_type=F32)
         cs = pl.ds(pl.multiple_of(half * HALF + c0, 128), n)
-
-        def body(i, _):
-            rows = pl.ds(pl.multiple_of(i * 16, 16), 16)
-            g = gate_ref[rows, cs].astype(F32)
-            u = up_ref[rows, cs].astype(F32)
-            h = hg[rows, 0:n]
-            s = jax.nn.sigmoid(g)
-            gg_ref[rows, cs] = (h * u * s * (1.0 + g * (1.0 - s))).astype(BF)
-            ug_ref[rows, cs] = (h * g * s).astype(BF)
-            return 0
-
-        lax.fori_loop(0, TOK // 16, body, 0)
+        h = jnp.dot(og_ref[...], w_of(side, k, c0, n), preferred_element_type=F32)
+        gg_ref[:, cs] = (h * fg[half, :, pl.ds(c0, n)]).astype(BF)
+        ug_ref[:, cs] = (h * fu[half, :, pl.ds(c0, n)]).astype(BF)
 
     for side in K.co:
         for k in K.ABC:
@@ -624,7 +637,7 @@
     assert len(slots) <= NRECV and len(sent) <= NSEND, (len(slots), len(sent))
 
 
-NRECV, NSEND = 56, 20
+NRECV, NSEND = 58, 20
 
 GROUPS = {}
 for _first, _names in (
@@ -686,7 +699,8 @@
             V((TOK, D), BF),
             V((4, 256, 2 * TOK), BF),
             V((8, HALF), F32),
-            V((TOK, 512), F32),
+            V((2, TOK, HALF), F32),
+            V((2, TOK, HALF), F32),
             V((TOK, D), F32),
             V((16, HALF), F32),
             V((8, HALF), F32),
@@ -710,7 +724,7 @@
             pltpu.SemaphoreType.DMA((6,)),
         ],
         compiler_params=pltpu.CompilerParams(
-            collective_id=0, has_side_effects=True, vmem_limit_bytes=48_000_000
+            collective_id=0, has_side_effects=True, vmem_limit_bytes=56_000_000
         ),
     )(
         in_hbm(gate_pre.reshape(TOK, FF)),

time: 58 us -> 54.7 us (0.943)
  Pallas kernels: 57.3 us -> 54 us
    pallas_call x1, Pallas kernels: 55.5 us -> 52.2 us  [on_device(): pl.pallas_call(kernel, out_shape=(V((TOK, 512), BF), V((TOK, FF), BF), V(...]
where the time goes in v5:
time: 54.7 us; the launch traced here: 54.6 us
  Pallas kernels  54 us (99%)
  between operations  0.64 us (1%)
    pallas_call x1, Pallas kernels, on_device(): pl.pallas_call(kernel, out_shape=(V((TOK, 512), BF), V((TOK, FF), BF), V(...  52.2 us
    pallas_call x1, Pallas kernels, on_device(): pl.pallas_call(copy_kernel, out_shape=tuple((jax.ShapeDtypeStruct(o.shape...  1.79 us

profile of v5, /device:TPU:1, one launch (start us, length us, event | category | flops | bytes accessed | tf_op | source)
XLA Modules:
  0.0 54.6 jit_solution(11200053489649674968)
XLA Ops:
  0.6 52.2 %shard_map.109 = (bf16[256,512]{1,0:T(8,128)(2,1)S(1)}, bf16[256,2816]{1,0:T(8,128)(2,1)S(1)}, bf16[256,2816]{1,0:T(8,128)(2,1)S(1)}, f32[8,2816]{1,0:T(8,128)S(...) custom-call(bf16[256,2816]{1,0:T(8,128)(2,1)} %bitcast.6, bf16[256,2816]{1,0:T(8,128)(2,1)} %bitcast.7, ...), custom_call_target="tpu_custom_call" | custom-call | tf_op jit(solution)/shard_map/pallas_call | solution.py:680
  52.8 1.8 %shard_map.110 = (bf16[256,512]{1,0:T(8,128)(2,1)}, bf16[256,2816]{1,0:T(8,128)(2,1)}, bf16[256,2816]{1,0:T(8,128)(2,1)}, f32[8,2816]{1,0:T(8,128)}, f32[8,2816]{1,0:T(8,128)}, /*index=5*/f32[8,2816]{1,0:T(8,128)}) custom-call(bf16[256,512]{1,0:T(8,128)(2,1)S(1)} %get-tuple-element.18.refs_0_, bf16[256,2816]{1,0:T(8,128)(2,1)S(1)} %get-tuple-element.19.refs_1_, ...), custom_call_target="tpu_custom_call" | custom-call | tf_op jit(solution)/shard_map/pallas_call | solution.py:737

commit v6 on v5

--- a/solution.py
+++ b/solution.py
@@ -38,45 +38,53 @@
 K = Names()
 
 ORDER = (
-    K.init, K.hidO_, K.hid2_, K.gp, K.gC0, K.gC1, K.RC1, K.A1, K.gB0, K.gB1, K.RB1, K.gA0,
-    K.gA1, K.RA1, K.A2, K.RA2L0, K.BC1, K.RA3R1, K.A3_1L0, K.A3_1R1, K.RA2L1, K.RA3L0, K.A3_1R0,
-    K.C2R, K.C2L, K.fc, K.A3_1L1, K.B2, K.RA3R0, K.RB2L, K.A3_2L0, K.A3_2L1, K.A3_2R1, K.RA4R0,
-    K.A3_2R0, K.B3R, K.B3L, K.RC2, K.C3, K.A3_3L0, K.fo, K.A3_3L1, K.RA3L1, K.RB2R, K.RB3,
-    K.RC2b, K.RC2c, K.C4, K.hg_cC0, K.RA4R1, K.lo_cC, K.RC3R, K.RA4L0, K.A6, K.B4, K.lo_oC,
-    K.lo_cA, K.RA4L1, K.lo_cB, K.lo_oA, K.RB4, K.lo_oB, K.losend, K.RC3L, K.hg_oB0, K.hg_oA1,
-    K.RA5, K.RC4, K.hg_cA1, K.hg_oB1, K.hg_cB0, K.hg_oC0, K.hg_cC1, K.RA6, K.hg_cA0, K.hg_cB1,
-    K.RB5, K.hg_oA0, K.RA7, K.RC5, K.fin_, K.hg_oC1, K.lofin, K.adam,
+    K.init, K.hidO_, K.hid2_, K.gp, K.gB0, K.A1, K.gC0, K.gC1, K.RC1, K.gB1, K.RB1, K.gA0,
+    K.gA1, K.RA1, K.A2, K.BC1N, K.A3_1L0, K.A3_1L1, K.RA2L0, K.BC1F, K.A3_2L0, K.RB2L, K.A3_1R0,
+    K.A3_1R1, K.B2N, K.RA3R0, K.fo, K.C2RF, K.A3_2L1, K.C2RN, K.C2LN, K.RA2L1, K.A3_2R0, K.B3RF,
+    K.C2LF, K.A3_3L0, K.A3_3L1, K.B2F, K.B3RN, K.fc, K.RA3L0, K.A3_2R1, K.RA3R1, K.C3N, K.RA4R0,
+    K.B3LN, K.C3F, K.RB2R, K.RB3, K.B3LF, K.RA3L1, K.A6, K.RC2, K.lo_cA, K.C4, K.lo_cC,
+    K.hg_cC0, K.RA4L0, K.B4, K.lo_cB, K.lo_oA, K.RA4R1, K.RC2b, K.hg_cC1, K.RC2c, K.RA4L1,
+    K.lo_oC, K.lo_oB, K.RB4, K.losend, K.RC3R, K.RC3L, K.hg_cA1, K.hg_cB1, K.hg_cA0, K.hg_oB1,
+    K.hg_oA1, K.RA5, K.RC4, K.RA6, K.hg_cB0, K.hg_oC1, K.hg_oC0, K.RB5, K.hg_oA0, K.hg_oB0,
+    K.RA7, K.RC5, K.fin_, K.lofin, K.adam,
 )
 ORDS = {
-    K.init: (K.Zd7, K.Zd5, K.Zd6, K.Zd1, K.Ax, K.og, K.Zd3, K.Zd4, K.Zd2,),
-    K.A1: (K.Ay3, K.Ay1, K.Ay2,),
-    K.A2: (K.Az1L0, K.DA0, K.Az1R1, K.Az1L1, K.Az1R0,),
+    K.init: (K.Zd4, K.Ax, K.Zd5, K.Zd2, K.Zd1, K.Zd3, K.Zd7, K.Zd6, K.og,),
+    K.A1: (K.Ay1, K.Ay2, K.Ay3,),
+    K.A2: (K.Az1R0, K.DA0, K.Az1L0, K.Az1L1, K.Az1R1,),
     K.A3_1R0: (K.DA1R0, K.Az2R0,),
     K.A3_1R1: (K.DA1R1, K.Az2R1,),
     K.A3_1L0: (K.DA1L0, K.Az2L0,),
-    K.A3_1L1: (K.Az2L1, K.DA1L1,),
-    K.A3_2R0: (K.Az3R0, K.DA2R0,),
+    K.A3_1L1: (K.DA1L1, K.Az2L1,),
+    K.A3_2R0: (K.DA2R0, K.Az3R0,),
     K.A3_2R1: (K.Az3R1, K.DA2R1,),
     K.A3_2L0: (K.DA2L0, K.Az3L0,),
     K.A3_2L1: (K.DA2L1, K.Az3L1,),
     K.A3_3L0: (K.Az4L0, K.DA3L0,),
-    K.A3_3L1: (K.Az4L1, K.DA3L1,),
-    K.BC1: (K.Bx, K.Cy1L, K.DC0, K.Cx0, K.DB0, K.By1Lx, K.Cy1R, K.By1Rx,),
-    K.B2: (K.By1Ro, K.DB1, K.By1Lo,),
-    K.B3R: (K.By2R, K.DB2,),
-    K.B3L: (K.By2L, K.DB3,),
-    K.C2R: (K.Cx3, K.DC3, K.Cy2R,),
-    K.C2L: (K.DC1, K.Cy2L, K.Cx1,),
-    K.C3: (K.Cx2, K.DC2,),
-    K.RC1: (K.rCx0, K.rCx2, K.rCx1, K.rCx3,),
-    K.RB1: (K.rB1L, K.rB2R1, K.rB2L1, K.rB1R,),
-    K.RA1: (K.rA1L0, K.rA2R1, K.rA1L1, K.rA2R0,),
+    K.A3_3L1: (K.DA3L1, K.Az4L1,),
+    K.BC1N: (K.DB0N, K.Cy1RN, K.Cy1LN, K.DC0N, K.BxN, K.By1LxN, K.Cx0N, K.By1RxN,),
+    K.B2N: (K.By1LoN, K.DB1N, K.By1RoN,),
+    K.B3RN: (K.By2RN, K.DB2N,),
+    K.B3LN: (K.DB3N, K.By2LN,),
+    K.C2RN: (K.Cx3N, K.DC3N, K.Cy2RN,),
+    K.C2LN: (K.Cx1N, K.DC1N,),
+    K.C3N: (K.Cx2N, K.DC2N,),
+    K.BC1F: (K.BxF, K.Cy1RF, K.DC0F, K.Cx0F, K.By1RxF, K.DB0F, K.By1LxF, K.Cy1LF,),
+    K.B2F: (K.By1LoF, K.DB1F, K.By1RoF,),
+    K.B3RF: (K.DB2F, K.By2RF,),
+    K.B3LF: (K.DB3F, K.By2LF,),
+    K.C2RF: (K.Cx3F, K.DC3F,),
+    K.C2LF: (K.Cx1F, K.DC1F, K.Cy2LF,),
+    K.C3F: (K.Cx2F, K.DC2F,),
+    K.RC1: (K.rCx1, K.rCx2, K.rCx0, K.rCx3,),
+    K.RB1: (K.rB2L1, K.rB1L, K.rB1R, K.rB2R1,),
+    K.RA1: (K.rA2R0, K.rA1L0, K.rA1L1, K.rA2R1,),
     K.RA5: (K.rAy2, K.rAy1, K.rAy3,),
-    K.RB4: (K.rBz1, K.rBz5, K.rBz6, K.rBz7, K.rBz2, K.rBz3, K.rBz4,),
-    K.RC2: (K.rCy1R, K.rCy1L,),
-    K.RC4: (K.rCz7, K.rCz6, K.rCz4, K.rCz3, K.rCz1, K.rCz2, K.rCz5,),
+    K.RB4: (K.rBz6, K.rBz3, K.rBz2, K.rBz7, K.rBz1, K.rBz4, K.rBz5,),
+    K.RC2: (K.rCy1L, K.rCy1R,),
+    K.RC4: (K.rCz4, K.rCz6, K.rCz7, K.rCz3, K.rCz2, K.rCz1, K.rCz5,),
 }
-HORDER = (K.C, K.B, K.A)
+HORDER = (K.B, K.C, K.A)
 
 
 def kernel(
@@ -161,10 +169,13 @@
         for n in names:
             table[n]
         for name in list(names) + [n for n in table if n not in names]:
-            _, src, dst, dev = table[name]
-            rc(name, src, dst, dev).start()
-            sent[size(src)] += 1
-            arriving[group_of(name)] = arriving.get(group_of(name), 0) + size(dst)
+            _, srcs, dsts, dev = table[name]
+            if not isinstance(srcs, list):
+                srcs, dsts = [srcs], [dsts]
+            for src, dst in zip(srcs, dsts):
+                rc(name, src, dst, dev).start()
+                sent[size(src)] += 1
+                arriving[group_of(name)] = arriving.get(group_of(name), 0) + size(dst)
 
     def recv(name, dst, dev):
         with jax.named_scope(K.wait_ + name):
@@ -297,63 +308,70 @@
     def cref(yi, xi, zs=allr):
         return Wb(yi, xi, zs, allr, cols(C))
 
-    @step
-    def BC1():
-        recv_all(K.Zd)
-        b, cc = bref(y, x), cref(y, x)
-        sends(K.BC1, [
-            same(K.Bx, b, dx), same(K.By1Rx, b, dy(1)), same(K.By1Lx, b, dy(-1)),
-            same(K.Cy1R, cc, dy(1)), same(K.Cy1L, cc, dy(-1)), same(K.Cx0, cc, dx),
-            same(K.DB0, b, dc), same(K.DC0, cc, dc),
-        ])
-
-    @step
-    def B2():
-        b = bref(y, ox)
-        recv(K.Bx, b, dx)
-        sends(K.B2, [same(K.By1Ro, b, dy(1)), same(K.By1Lo, b, dy(-1)), same(K.DB1, b, dc)])
-
-    @step
-    def B3R():
-        b = bref(yy(-1), x)
-        recv(K.By1Rx, b, dy(-1))
-        sends(K.B3R, [same(K.By2R, b, dy(1)), same(K.DB2, b, dc)])
-
-    @step
-    def B3L():
-        b = bref(yy(1), ox)
-        recv(K.By1Lo, b, dy(1))
-        sends(K.B3L, [same(K.By2L, b, dy(-1)), same(K.DB3, b, dc)])
-
-    last_b = ((K.By2R, 2, x, -1), (K.By2L, 2, ox, 1), (K.By1Ro, -1, ox, -1), (K.By1Lx, 1, x, 1))
+    zones = {K.N: (0, 1, -1, 2, -2), K.F: (3, -3, 4)}
+
+    def bblk(yi, xi, p):
+        return [Wb(yi, xi, zz(o), allr, cols(B)) for o in zones[p]]
+
+    def cblk(yi, xi, p):
+        return [Wb(yi, xi, zz(o), allr, cols(C)) for o in zones[p]]
+
+    def bc_steps(p):
+        def BC1():
+            recv_all(K.Zd + p)
+            b, cc = bblk(y, x, p), cblk(y, x, p)
+            sends(K.BC1 + p, [
+                same(K.Bx + p, b, dx), same(K.By1Rx + p, b, dy(1)), same(K.By1Lx + p, b, dy(-1)),
+                same(K.Cy1R + p, cc, dy(1)), same(K.Cy1L + p, cc, dy(-1)), same(K.Cx0 + p, cc, dx),
+                same(K.DB0 + p, b, dc), same(K.DC0 + p, cc, dc),
+            ])
+
+        def B2():
+            recv_all(K.Bx + p)
+            b = bblk(y, ox, p)
+            sends(K.B2 + p, [
+                same(K.By1Ro + p, b, dy(1)), same(K.By1Lo + p, b, dy(-1)), same(K.DB1 + p, b, dc),
+            ])
+
+        def B3R():
+            recv_all(K.By1Rx + p)
+            b = bblk(yy(-1), x, p)
+            sends(K.B3R + p, [same(K.By2R + p, b, dy(1)), same(K.DB2 + p, b, dc)])
+
+        def B3L():
+            recv_all(K.By1Lo + p)
+            b = bblk(yy(1), ox, p)
+            sends(K.B3L + p, [same(K.By2L + p, b, dy(-1)), same(K.DB3 + p, b, dc)])
+
+        def C2R():
+            recv_all(K.Cy1R + p)
+            cc = cblk(yy(-1), x, p)
+            on = [same(K.Cy2RN, cc, dy(1))] if p == K.N else []
+            sends(K.C2R + p, on + [same(K.Cx3 + p, cc, dx), same(K.DC3 + p, cc, dc)])
+
+        def C2L():
+            recv_all(K.Cy1L + p)
+            cc = cblk(yy(1), x, p)
+            on = [same(K.Cy2LF, cc, dy(-1))] if p == K.F else []
+            sends(K.C2L + p, on + [same(K.Cx1 + p, cc, dx), same(K.DC1 + p, cc, dc)])
+
+        def C3():
+            recv_all(K.Cy2RN if p == K.N else K.Cy2LF)
+            cc = cblk(yy(2), x, p)
+            sends(K.C3 + p, [same(K.Cx2 + p, cc, dx), same(K.DC2 + p, cc, dc)])
+
+        for f in (BC1, B2, B3R, B3L, C2R, C2L, C3):
+            S[f.__name__ + p] = f
+
+    bc_steps(K.N)
+    bc_steps(K.F)
+    last_b = ((K.By2R, 2, x), (K.By2L, 2, ox), (K.By1Ro, -1, ox), (K.By1Lx, 1, x))
+    lo4, hi4 = pl.ds(0, 4), pl.ds(4, 4)
 
     @step
     def B4():
         recv_all(K.By9)
-        sends(K.B4, [same(K.D + nm, bref(yy(o), xi), dc) for nm, o, xi, d in last_b])
-
-    lo4, hi4 = pl.ds(0, 4), pl.ds(4, 4)
-
-    @step
-    def C2R():
-        recv(K.Cy1R, cref(yy(-1), x), dy(-1))
-        sends(K.C2R, [
-            same(K.Cy2R, cref(yy(-1), x, lo4), dy(1)),
-            same(K.Cx3, cref(yy(-1), x), dx), same(K.DC3, cref(yy(-1), x), dc),
-        ])
-
-    @step
-    def C2L():
-        recv(K.Cy1L, cref(yy(1), x), dy(1))
-        sends(K.C2L, [
-            same(K.Cy2L, cref(yy(1), x, hi4), dy(-1)),
-            same(K.Cx1, cref(yy(1), x), dx), same(K.DC1, cref(yy(1), x), dc),
-        ])
-
-    @step
-    def C3():
-        recv_all(K.Cy2)
-        sends(K.C3, [same(K.Cx2, cref(yy(2), x), dx), same(K.DC2, cref(yy(2), x), dc)])
+        sends(K.B4, [same(K.D + nm, bref(yy(o), xi), dc) for nm, o, xi in last_b])
 
     @step
     def C4():
@@ -637,16 +655,17 @@
     assert len(slots) <= NRECV and len(sent) <= NSEND, (len(slots), len(sent))
 
 
-NRECV, NSEND = 58, 20
+NRECV, NSEND = 64, 21
 
 GROUPS = {}
 for _first, _names in (
     (K.Az9, (K.Az3R0, K.Az3R1, K.Az4L0, K.Az4L1)),
-    (K.By9, (K.By2R, K.By2L, K.By1Ro, K.By1Lx)),
+    (K.By9, tuple(a + b for a in (K.By2R, K.By2L, K.By1Ro, K.By1Lx) for b in K.NF)),
+    (K.ZdN, (K.Zd1, K.Zd2, K.Zd6, K.Zd7)),
+    (K.ZdF, (K.Zd3, K.Zd4, K.Zd5)),
     (K.rB4, (K.rB2R0, K.rB2L1, K.rBx)),
     (K.rB3, (K.rB2R1, K.rB2L0)),
     (K.rC4, (K.rCx0, K.rCy2R0, K.rCy2R1, K.rCy2L0, K.rCy2L1)),
-    (K.Cy2, (K.Cy2R, K.Cy2L)),
 ):
     for _n in _names:
         GROUPS[_n] = _first
@@ -655,7 +674,7 @@
 def group_of(name):
     if name in GROUPS:
         return GROUPS[name]
-    for p in (K.Zd, K.Ay, K.rAy, K.rBz, K.rCz, K.DA, K.DB, K.DC, K.Cx, K.rA4):
+    for p in (K.Ay, K.rAy, K.rBz, K.rCz, K.DA, K.DB, K.DC, K.Cx, K.rA4):
         if name.startswith(p):
             return p
     return name

time: 54.7 us -> 55.5 us (1.015)
  Pallas kernels: 54 us -> 54.8 us
    pallas_call x1, Pallas kernels: 52.2 us -> 53 us  [on_device(): pl.pallas_call(kernel, out_shape=(V((TOK, 512), BF), V((TOK, FF), BF), V(...]
where the time goes in v6:
time: 55.5 us; the launch traced here: 55.4 us
  Pallas kernels  54.8 us (99%)
  between operations  0.64 us (1%)
    pallas_call x1, Pallas kernels, on_device(): pl.pallas_call(kernel, out_shape=(V((TOK, 512), BF), V((TOK, FF), BF), V(...  53 us
    pallas_call x1, Pallas kernels, on_device(): pl.pallas_call(copy_kernel, out_shape=tuple((jax.ShapeDtypeStruct(o.shape...  1.79 us

profile of v6, /device:TPU:1, one launch (start us, length us, event | category | flops | bytes accessed | tf_op | source)
XLA Modules:
  0.0 55.4 jit_solution(5368695405938906662)
XLA Ops:
  0.6 53.0 %shard_map.109 = (bf16[256,512]{1,0:T(8,128)(2,1)S(1)}, bf16[256,2816]{1,0:T(8,128)(2,1)S(1)}, bf16[256,2816]{1,0:T(8,128)(2,1)S(1)}, f32[8,2816]{1,0:T(8,128)S(...) custom-call(bf16[256,2816]{1,0:T(8,128)(2,1)} %bitcast.6, bf16[256,2816]{1,0:T(8,128)(2,1)} %bitcast.7, ...), custom_call_target="tpu_custom_call" | custom-call | tf_op jit(solution)/shard_map/pallas_call | solution.py:699
  53.6 1.8 %shard_map.110 = (bf16[256,512]{1,0:T(8,128)(2,1)}, bf16[256,2816]{1,0:T(8,128)(2,1)}, bf16[256,2816]{1,0:T(8,128)(2,1)}, f32[8,2816]{1,0:T(8,128)}, f32[8,2816]{1,0:T(8,128)}, /*index=5*/f32[8,2816]{1,0:T(8,128)}) custom-call(bf16[256,512]{1,0:T(8,128)(2,1)S(1)} %get-tuple-element.18.refs_0_, bf16[256,2816]{1,0:T(8,128)(2,1)S(1)} %get-tuple-element.19.refs_1_, ...), custom_call_target="tpu_custom_call" | custom-call | tf_op jit(solution)/shard_map/pallas_call | solution.py:756

commit v7 on v5

--- a/solution.py
+++ b/solution.py
@@ -38,14 +38,13 @@
 K = Names()
 
 ORDER = (
-    K.init, K.hidO_, K.hid2_, K.gp, K.gC0, K.gC1, K.RC1, K.A1, K.gB0, K.gB1, K.RB1, K.gA0,
-    K.gA1, K.RA1, K.A2, K.RA2L0, K.BC1, K.RA3R1, K.A3_1L0, K.A3_1R1, K.RA2L1, K.RA3L0, K.A3_1R0,
-    K.C2R, K.C2L, K.fc, K.A3_1L1, K.B2, K.RA3R0, K.RB2L, K.A3_2L0, K.A3_2L1, K.A3_2R1, K.RA4R0,
-    K.A3_2R0, K.B3R, K.B3L, K.RC2, K.C3, K.A3_3L0, K.fo, K.A3_3L1, K.RA3L1, K.RB2R, K.RB3,
-    K.RC2b, K.RC2c, K.C4, K.hg_cC0, K.RA4R1, K.lo_cC, K.RC3R, K.RA4L0, K.A6, K.B4, K.lo_oC,
-    K.lo_cA, K.RA4L1, K.lo_cB, K.lo_oA, K.RB4, K.lo_oB, K.losend, K.RC3L, K.hg_oB0, K.hg_oA1,
-    K.RA5, K.RC4, K.hg_cA1, K.hg_oB1, K.hg_cB0, K.hg_oC0, K.hg_cC1, K.RA6, K.hg_cA0, K.hg_cB1,
-    K.RB5, K.hg_oA0, K.RA7, K.RC5, K.fin_, K.hg_oC1, K.lofin, K.adam,
+    K.init, K.hidO_, K.hid2_, K.gp, K.gC0, K.RC1, K.A1, K.gB0, K.RB1, K.gA0, K.RA1, K.A2,
+    K.RA2L0, K.BC1, K.RA3R1, K.A3_1L0, K.A3_1R1, K.RA2L1, K.RA3L0, K.A3_1R0, K.C2R, K.C2L, K.fc,
+    K.A3_1L1, K.B2, K.RA3R0, K.RB2L, K.A3_2L0, K.A3_2L1, K.A3_2R1, K.RA4R0, K.A3_2R0, K.B3R,
+    K.B3L, K.RC2, K.C3, K.A3_3L0, K.fo, K.A3_3L1, K.RA3L1, K.RB2R, K.RB3, K.RC2b, K.RC2c, K.C4,
+    K.RA4R1, K.lo_cC, K.RC3R, K.RA4L0, K.A6, K.B4, K.lo_oC, K.lo_cA, K.RA4L1, K.lo_cB, K.lo_oA,
+    K.RB4, K.lo_oB, K.losend, K.RC3L, K.hg_oB0, K.hg_oA0, K.RA5, K.RC4, K.hg_cA0, K.hg_cB0,
+    K.hg_oC0, K.hg_cC0, K.RA6, K.RB5, K.RA7, K.RC5, K.fin_, K.lofin, K.adam,
 )
 ORDS = {
     K.init: (K.Zd7, K.Zd5, K.Zd6, K.Zd1, K.Ax, K.og, K.Zd3, K.Zd4, K.Zd2,),
@@ -370,15 +369,15 @@
         cr = ranges[k]
         if j == 0:
             recv(K.h + k, hid2.at[pl.ds(TOK, TOK), cols(cr)], dc)
-        c0 = cr[0] + 256 * j
-        n = min(256, cr[1] - 256 * j)
+        c0 = cr[0] + 512 * j
+        n = min(512, cr[1] - 512 * j)
         p = jnp.dot(
             ogT[...].reshape(D, 2 * TOK), hid2[:, pl.ds(c0, n)], preferred_element_type=F32
         )
         G[:, :, :, :, pl.ds(c0, n)] = p.reshape(NY, NX, NZ, 16, n)
 
     for k in K.ABC:
-        for j in range(-(-ranges[k][1] // 256)):
+        for j in range(-(-ranges[k][1] // 512)):
             S[f"g{k}{j}"] = lambda k=k, j=j: grads(k, j)
 
     def ga(h, zi):
@@ -570,8 +569,8 @@
         started.append(1)
 
     def hgrad(side, k, j):
-        c0 = ranges[k][0] + 256 * j
-        n = min(256, ranges[k][1] - 256 * j)
+        c0 = ranges[k][0] + 512 * j
+        n = min(512, ranges[k][1] - 512 * j)
         half = c if side == K.c else oc
         cs = pl.ds(pl.multiple_of(half * HALF + c0, 128), n)
         h = jnp.dot(og_ref[...], w_of(side, k, c0, n), preferred_element_type=F32)
@@ -581,7 +580,7 @@
     for side in K.co:
         for k in K.ABC:
             S[f"lo_{side}{k}"] = lambda side=side, k=k: lo(side, k)
-            for j in range(-(-ranges[k][1] // 256)):
+            for j in range(-(-ranges[k][1] // 512)):
                 S[f"hg_{side}{k}{j}"] = lambda side=side, k=k, j=j: hgrad(side, k, j)
 
     @step

time: 54.7 us -> 54.5 us (level)
  no operation moved by 1% of the time
where the time goes in v7:
time: 54.5 us; the launch traced here: 54.4 us
  Pallas kernels  53.8 us (99%)
  between operations  0.64 us (1%)
    pallas_call x1, Pallas kernels, on_device(): pl.pallas_call(kernel, out_shape=(V((TOK, 512), BF), V((TOK, FF), BF), V(...  52 us
    pallas_call x1, Pallas kernels, on_device(): pl.pallas_call(copy_kernel, out_shape=tuple((jax.ShapeDtypeStruct(o.shape...  1.79 us

profile of v7, /device:TPU:1, one launch (start us, length us, event | category | flops | bytes accessed | tf_op | source)
XLA Modules:
  0.0 54.4 jit_solution(2822641004482285873)
XLA Ops:
  0.6 52.0 %shard_map.109 = (bf16[256,512]{1,0:T(8,128)(2,1)S(1)}, bf16[256,2816]{1,0:T(8,128)(2,1)S(1)}, bf16[256,2816]{1,0:T(8,128)(2,1)S(1)}, f32[8,2816]{1,0:T(8,128)S(...) custom-call(bf16[256,2816]{1,0:T(8,128)(2,1)} %bitcast.6, bf16[256,2816]{1,0:T(8,128)(2,1)} %bitcast.7, ...), custom_call_target="tpu_custom_call" | custom-call | tf_op jit(solution)/shard_map/pallas_call | solution.py:679
  52.6 1.8 %shard_map.110 = (bf16[256,512]{1,0:T(8,128)(2,1)}, bf16[256,2816]{1,0:T(8,128)(2,1)}, bf16[256,2816]{1,0:T(8,128)(2,1)}, f32[8,2816]{1,0:T(8,128)}, f32[8,2816]{1,0:T(8,128)}, /*index=5*/f32[8,2816]{1,0:T(8,128)}) custom-call(bf16[256,512]{1,0:T(8,128)(2,1)S(1)} %get-tuple-element.18.refs_0_, bf16[256,2816]{1,0:T(8,128)(2,1)S(1)} %get-tuple-element.19.refs_1_, ...), custom_call_target="tpu_custom_call" | custom-call | tf_op jit(solution)/shard_map/pallas_call | solution.py:736
